TPU v7x, 32 devices: a whole 2x2x4 slice. The times are simulated.
32 devices in a mesh: lat: 4 (over z), lon: 8 (over y, x, core).
Axes of the slice: x: 2, y: 2, z: 4, core: 2. Of those that a mesh axis runs over, the one named last changes fastest.
Arguments:
- zonal_wind: float32 [32, 32, 2048], P(None, 'lat', 'lon'), may hold values from -6 to 6
- merid_wind: float32 [32, 32, 2048], P(None, 'lat', 'lon'), may hold values from -6 to 6
- vertical_wind: float32 [32, 32, 2048], P(None, 'lat', 'lon'), may hold values from -6 to 6
- pressure: float32 [32, 32, 2048], P(None, 'lat', 'lon'), may hold values from -6 to 6
- zonal_coef: float32 [32], P('lat'), may hold values from 0.05 to 0.4
- merid_coef: float32 [32], P('lat'), may hold values from 0.05 to 0.4
- level_coef: float32 [32], replicated, may hold values from 0.3 to 1.5
- sound_coef: float32 [32, 32, 2048], P(None, 'lat', 'lon'), may hold values from 0.2 to 2
- cutoff: int32 [32], replicated, may hold values from 1 to 511
- filter_mask: int32 [32], replicated, may hold values from 0 to 1, as said below
Outputs:
- zonal_next: float32 [32, 32, 2048], P(None, 'lat', 'lon')
- merid_next: float32 [32, 32, 2048], P(None, 'lat', 'lon')
- vertical_next: float32 [32, 32, 2048], P(None, 'lat', 'lon')
- pressure_next: float32 [32, 32, 2048], P(None, 'lat', 'lon')
Inputs may be any that keep to these rules, and one draw needn't show every extreme that they name: `filter_mask`: for every latitude j below 16 exactly one of j and j + 16 is filtered; the filtered ones are the first n and the last 16 - n latitudes, for some n from 4 to 12.
All inputs are finite; a program needn't handle non-finite values.
Results may differ from a plain program's by a relative error of at most 0.0001.
Values sent between devices are 32-bit elements; how exact they have to be, the bound alone decides.
A program may use at most 64 MiB of HBM per device.

v0:
```python
import functools
import math

import ml_dtypes
import numpy as np
import jax
import jax.numpy as jnp
from jax import lax
from jax.experimental import pallas as pl
from jax.experimental.pallas import tpu as pltpu
from jax.sharding import PartitionSpec as P

SUBSTEPS = 2
FUSED_VMEM = 40 * 2 ** 20
FINISH_VMEM = 4 * 2 ** 20


def extended(block, sides, width):
    for axis, dim in sides:
        count = lax.axis_size(axis)
        forward = [(i, i + 1) for i in range(count - 1)]
        forward.append((count - 1, 0))
        backward = [(target, source) for source, target in forward]
        low = lax.ppermute(
            lax.slice_in_dim(block, block.shape[dim] - width, None, axis=dim), axis, forward
        )
        high = lax.ppermute(lax.slice_in_dim(block, 0, width, axis=dim), axis, backward)
        block = jnp.concatenate([low, block, high], axis=dim)
    return block


def rim_fix(padded, lat_dim):
    band_index = lax.axis_index("lat")
    bands = lax.axis_size("lat")
    extent = padded.shape[lat_dim]
    position = lax.broadcasted_iota(jnp.int32, padded.shape, lat_dim)
    first_edge = jnp.logical_and(position == 0, band_index == 0)
    final_edge = jnp.logical_and(position == extent - 1, band_index == bands - 1)
    return jnp.where(jnp.logical_or(first_edge, final_edge), 0.0, padded)


def dft_tables(length):
    half_len = length // 2
    sample = lax.broadcasted_iota(jnp.int32, (length, length), 0)
    column = lax.broadcasted_iota(jnp.int32, (length, length), 1)
    is_cosine = column <= half_len
    wavenum = jnp.where(is_cosine, column, column - half_len)
    phase = sample * wavenum % length
    angle = 2.0 * math.pi / length * phase.astype(jnp.float32)
    forward = jnp.where(is_cosine, jnp.cos(angle), jnp.sin(angle))
    single = jnp.logical_and(is_cosine, jnp.logical_or(wavenum == 0, wavenum == half_len))
    weight = jnp.where(single, 1.0, 2.0) / length
    inverse = jnp.transpose(forward * weight)
    wave_row = wavenum[0].astype(jnp.float32)
    return (forward, inverse, wave_row)


def damping(wave_row, limits):
    bound_col = limits[:, None]
    ratio = bound_col / jnp.maximum(wave_row[None, :], 1.0)
    return jnp.where(wave_row[None, :] > bound_col, ratio * ratio, 1.0)


def transform_band(block, limits, forward, inverse, wave_row):
    circles = lax.all_to_all(block, "lon", split_axis=1, concat_axis=3, tiled=True)
    spectra = jnp.einsum("vetj,jc->vetc", circles, forward, precision=lax.Precision.HIGHEST)
    scaled = spectra * damping(wave_row, limits)
    damped = jnp.einsum("vetc,cj->vetj", scaled, inverse, precision=lax.Precision.HIGHEST)
    return lax.all_to_all(damped, "lon", split_axis=3, concat_axis=1, tiled=True)


def filtered_increments(increments, own_flags, own_limits, forward, inverse, wave_row):
    flag_cols = own_flags[:, None]
    damped = transform_band(increments, own_limits, forward, inverse, wave_row)
    return jnp.where(flag_cols, damped, increments)


def column_solve(vertical_wind, pstar, level_coef, sound_coef):
    levels = vertical_wind.shape[0]
    zero_slab = jnp.zeros_like(vertical_wind[0])
    ratios = []
    values = []
    prev_ratio = zero_slab
    prev_value = zero_slab
    for level in range(levels):
        alpha = level_coef[level]
        below = alpha * sound_coef[level]
        if level + 1 < levels:
            above = alpha * sound_coef[level + 1]
            rhs = vertical_wind[level] - alpha * (pstar[level + 1] - pstar[level])
        else:
            above = zero_slab
            rhs = vertical_wind[level] + alpha * pstar[level]
        pivot = 1.0 + below + above + below * prev_ratio
        prev_ratio = -above / pivot
        prev_value = (rhs + below * prev_value) / pivot
        ratios.append(prev_ratio)
        values.append(prev_value)
    solved = [zero_slab] * levels
    upper_value = values[levels - 1]
    solved[levels - 1] = upper_value
    for level in range(levels - 2, -1, -1):
        upper_value = values[level] - ratios[level] * upper_value
        solved[level] = upper_value
    new_wind = jnp.stack(solved)
    wind_below = jnp.concatenate([zero_slab[None], new_wind[:-1]], axis=0)
    new_pressure = pstar - sound_coef * (new_wind - wind_below)
    return (new_wind, new_pressure)


def wide_body(
    zonal_wind,
    merid_wind,
    vertical_wind,
    pressure,
    zonal_coef,
    merid_coef,
    level_coef,
    sound_coef,
    cutoff,
    filter_mask,
):
    lat_rows = pressure.shape[1]
    start = lax.axis_index("lat") * lat_rows
    own_flags = lax.dynamic_slice_in_dim(filter_mask, start, lat_rows) > 0
    own_limits = lax.dynamic_slice_in_dim(cutoff, start, lat_rows).astype(jnp.float32)
    forward, inverse, wave_row = dft_tables(pressure.shape[2] * lax.axis_size("lon"))
    zonal_rows = zonal_coef[None, :, None]
    merid_rows = merid_coef[None, :, None]
    for step in range(SUBSTEPS):
        padded = extended(pressure, (("lat", 1), ("lon", 2)), 1)
        padded = rim_fix(padded, 1)
        zonal_step = -zonal_rows * (padded[:, 1:-1, 2:] - padded[:, 1:-1, :-2])
        merid_step = -merid_rows * (padded[:, 2:, 1:-1] - padded[:, :-2, 1:-1])
        increments = jnp.stack([zonal_step, merid_step])
        damped = filtered_increments(increments, own_flags, own_limits, forward, inverse, wave_row)
        winds = jnp.stack([zonal_wind, merid_wind]) + damped
        wind_pad = extended(winds, (("lat", 2), ("lon", 3)), 1)
        wind_pad = rim_fix(wind_pad, 2)
        diverge = zonal_rows * (wind_pad[0, :, 1:-1, 2:] - wind_pad[0, :, 1:-1, :-2])
        diverge = diverge + merid_rows * (wind_pad[1, :, 2:, 1:-1] - wind_pad[1, :, :-2, 1:-1])
        pstar = pressure - sound_coef * diverge
        vertical_wind, pressure = column_solve(vertical_wind, pstar, level_coef, sound_coef)
        zonal_wind = winds[0]
        merid_wind = winds[1]
    return (zonal_wind, merid_wind, vertical_wind, pressure)


LANE = 128
TILE = 2 * LANE


def circle_tables(length):
    blocks = length // LANE
    half = blocks // 2
    m = np.arange(LANE, dtype=np.float64)[:, None]
    tables = np.zeros((half, TILE, TILE))
    waves = np.zeros((half, TILE))
    c = np.arange(LANE)[None, :]
    low = np.where(c <= LANE // 2, np.cos(2 * np.pi * m * c / LANE), np.sin(2 * np.pi * m * (c - LANE // 2) / LANE))
    low = low * np.where((c == 0) | (c == LANE // 2), np.sqrt(1.0 / LANE), np.sqrt(2.0 / LANE))
    k2 = np.arange(LANE // 2)[None, :]
    angle = 2 * np.pi * m * (half + blocks * k2) / length
    mid = np.concatenate([np.cos(angle), np.sin(angle)], axis=1) * np.sqrt(2.0 / LANE)
    tables[0, :LANE, :LANE] = low
    tables[0, LANE:, LANE:] = mid
    waves[0, :LANE] = blocks * np.where(c[0] <= LANE // 2, c[0], c[0] - LANE // 2)
    waves[0, LANE:] = np.tile(half + blocks * k2[0], 2)
    for k1 in range(1, half):
        k = k1 + blocks * c
        angle = 2 * np.pi * ((m * k) % length) / length
        cos, sin = np.cos(angle) / np.sqrt(LANE), np.sin(angle) / np.sqrt(LANE)
        tables[k1] = np.block([[cos, -sin], [sin, cos]])
        waves[k1] = np.tile(np.minimum(k[0], length - k[0]), 2)
    high = tables.astype(ml_dtypes.bfloat16)
    rest = (tables - high.astype(np.float64)).astype(ml_dtypes.bfloat16)
    scale = np.full((half, TILE), 2.0 / blocks)
    scale[0] = 1.0 / blocks
    rows = np.zeros((half, 8, TILE), np.float32)
    rows[:, 0] = waves
    rows[:, 1] = 4.0 * np.sin(2 * np.pi * waves / length) ** 2
    rows[:, 2] = scale
    return high, rest, rows


def split_parts(value):
    high = value.astype(jnp.bfloat16)
    rest = (value - high.astype(jnp.float32)).astype(jnp.bfloat16)
    return high, rest


def three_products(value, high_table, rest_table, transposed):
    high, rest = split_parts(value)
    dims = (((1,), (1 if transposed else 0,)), ((), ()))
    rows = value.shape[0]
    both = lax.dot_general(jnp.concatenate([high, rest], axis=0), high_table, dims, preferred_element_type=jnp.float32)
    corr = lax.dot_general(high, rest_table, dims, preferred_element_type=jnp.float32)
    return both[:rows] + (both[rows:] + corr)


def weighted(terms):
    total = None
    for coef, value in terms:
        if abs(coef) < 1e-12:
            continue
        if abs(abs(coef) - 1.0) < 1e-12:
            term = value
        else:
            term = abs(coef) * value
        if total is None:
            total = term if coef > 0 else -term
        else:
            total = total + term if coef > 0 else total - term
    return total


def coarse_forward(xs):
    count = len(xs)
    half = count // 2
    even = {b: xs[b] + xs[count - b] for b in range(1, half)}
    odd = {b: xs[b] - xs[count - b] for b in range(1, half)}
    real, imag = [], {}
    for k in range(half + 1):
        ends = xs[0] + xs[half] if k % 2 == 0 else xs[0] - xs[half]
        real.append(weighted([(1.0, ends)] + [(math.cos(2 * math.pi * b * k / count), even[b]) for b in range(1, half)]))
    for k in range(1, half):
        imag[k] = weighted([(-math.sin(2 * math.pi * b * k / count), odd[b]) for b in range(1, half)])
    pairs = [(real[0], real[half])] + [(real[k], imag[k]) for k in range(1, half)]
    return pairs


def coarse_inverse(pairs):
    half = len(pairs)
    count = 2 * half
    first, last = pairs[0]
    xs = [None] * count
    for b in range(half + 1):
        ends = first + last if b % 2 == 0 else first - last
        cos_part = weighted([(1.0, ends)] + [(math.cos(2 * math.pi * b * k / count), pairs[k][0]) for k in range(1, half)])
        if b in (0, half):
            xs[b] = cos_part
        else:
            sin_part = weighted([(-math.sin(2 * math.pi * b * k / count), pairs[k][1]) for k in range(1, half)])
            xs[b] = cos_part + sin_part
            xs[count - b] = cos_part - sin_part
    return xs


def to_spectrum(x_ref, high_ref, rest_ref, work_ref, spec_ref, units, per_band, accumulate):
    split = x_ref.shape[2] // LANE

    def one_unit(unit, carry):
        xs = [
            x_ref[d * units + unit, :, h * LANE:(h + 1) * LANE]
            for d in range(per_band)
            for h in range(split)
        ]
        for t, (left, right) in enumerate(coarse_forward(xs)):
            work_ref[t, unit, :, :LANE] = left
            work_ref[t, unit, :, LANE:] = right
        return carry

    lax.fori_loop(0, units, one_unit, 0)
    for t in range(high_ref.shape[0]):
        value = three_products(joined(work_ref[t]), high_ref[t], rest_ref[t], False)
        if accumulate:
            value = value + spec_ref[t]
        spec_ref[t] = value


def joined(value):
    return value.reshape((value.shape[0] * value.shape[1], value.shape[2]))


def circle_blocks(work_ref, band):
    pairs = [(work_ref[t, band, :, :LANE], work_ref[t, band, :, LANE:]) for t in range(work_ref.shape[0])]
    return coarse_inverse(pairs)


def put_blocks(out_ref, xs, unit, units):
    split = out_ref.shape[2] // LANE
    for b, value in enumerate(xs):
        out_ref[(b // split) * units + unit, :, (b % split) * LANE:(b % split + 1) * LANE] = value


def circle_diff(xs):
    count = len(xs)
    lane = lax.broadcasted_iota(jnp.int32, xs[0].shape, 1)
    ahead = [pltpu.roll(x, LANE - 1, 1) for x in xs]
    behind = [pltpu.roll(x, 1, 1) for x in xs]
    out = []
    for b in range(count):
        nxt = jnp.where(lane == LANE - 1, ahead[(b + 1) % count], ahead[b])
        prv = jnp.where(lane == 0, behind[(b - 1) % count], behind[b])
        out.append(nxt - prv)
    return out


def filter_values(limit, wave, scale):
    quotient = limit / jnp.maximum(wave, 1.0)
    return jnp.where(wave > limit, quotient * quotient, 1.0) * scale


def spectral_terms(spec_ref, t, units, rows_ref, own_ref, near_ref):
    rows = own_ref.shape[1]
    wave, sines, scale = rows_ref[t, 0:1, :], rows_ref[t, 1:2, :], rows_ref[t, 2:3, :]
    zonal = own_ref[0, :, 0:1]
    merid = own_ref[1, :, 0:1]
    factor = filter_values(own_ref[2, :, 0:1], wave, scale)
    south = near_ref[0, 1, rows - 1:rows, 0:1] * filter_values(near_ref[0, 2, rows - 1:rows, 0:1], wave, scale)
    north = near_ref[1, 1, 0:1, 0:1] * filter_values(near_ref[1, 2, 0:1, 0:1], wave, scale)
    row = lax.broadcasted_iota(jnp.int32, (rows, TILE), 0)
    around = merid * factor
    along = (zonal * zonal) * sines * factor
    smooth, v_parts, d_parts = [], [], []
    for l in range(units):
        own = spec_ref[t, l * rows:(l + 1) * rows, :]
        below = spec_ref[t, units * rows + 2 * l:units * rows + 2 * l + 2, :]
        above = spec_ref[t, (units + 1) * rows + 2 * l:(units + 1) * rows + 2 * l + 2, :]
        upper = jnp.where(row == rows - 1, above[0:1], pltpu.roll(own, rows - 1, 0))
        lower = jnp.where(row == 0, below[1:2], pltpu.roll(own, 1, 0))
        mid = -around * (upper - lower)
        v_south = -south * (own[0:1] - below[0:1])
        v_north = -north * (above[1:2] - own[rows - 1:rows])
        upper = jnp.where(row == rows - 1, v_north, pltpu.roll(mid, rows - 1, 0))
        lower = jnp.where(row == 0, v_south, pltpu.roll(mid, 1, 0))
        smooth.append(factor * own)
        v_parts.append(mid)
        d_parts.append(along * own + merid * (upper - lower))
    return smooth, v_parts, d_parts


def factor_columns(a_ref, s_ref, ratio_ref, inv_ref):
    levels = s_ref.shape[0]
    prev = jnp.zeros(s_ref.shape[1:], jnp.float32)
    for level in range(levels):
        alpha = a_ref[level]
        below = alpha * s_ref[level]
        above = alpha * s_ref[level + 1] if level + 1 < levels else jnp.zeros_like(below)
        inv = 1.0 / (1.0 + below + above + below * prev)
        prev = -above * inv
        ratio_ref[level] = prev
        inv_ref[level] = inv


def solve_columns(a_ref, s_ref, w_ref, p_ref, base_ref, d_ref, ratio_ref, inv_ref, w_out, p_out):
    levels = s_ref.shape[0]

    def star(level):
        return p_ref[level] - s_ref[level] * (base_ref[level] + d_ref[level])

    here = star(0)
    prev = jnp.zeros_like(here)
    for level in range(levels):
        alpha = a_ref[level]
        p_out[level] = here
        if level + 1 < levels:
            nxt = star(level + 1)
            rhs = w_ref[level] - alpha * (nxt - here)
        else:
            nxt = here
            rhs = w_ref[level] + alpha * here
        prev = (rhs + alpha * s_ref[level] * prev) * inv_ref[level]
        w_out[level] = prev
        here = nxt
    upper = w_out[levels - 1]
    for level in range(levels - 1, 0, -1):
        lower = w_out[level - 1] - ratio_ref[level - 1] * upper
        w_out[level - 1] = lower
        p_out[level] = p_out[level] - s_ref[level] * (upper - lower)
        upper = lower
    p_out[0] = p_out[0] - s_ref[0] * upper


def base_divergence(u_ref, v_ref, own_ref, west_ref, east_ref, south_ref, north_ref, base_ref, is_first, is_last):
    zonal = own_ref[0][:, 0:1]
    merid = own_ref[1][:, 0:1]
    rows, width = u_ref.shape[1:]
    lane = lax.broadcasted_iota(jnp.int32, (rows, width), 1)
    row = lax.broadcasted_iota(jnp.int32, (rows, width), 0)
    keep_south = jnp.where(is_first, 0.0, 1.0)
    keep_north = jnp.where(is_last, 0.0, 1.0)
    west = west_ref[...]
    east = east_ref[...]
    for level in range(u_ref.shape[0]):
        u = u_ref[level]
        v = v_ref[level]
        ahead = jnp.where(lane == width - 1, east[:, level:level + 1], pltpu.roll(u, width - 1, 1))
        behind = jnp.where(lane == 0, west[:, level:level + 1], pltpu.roll(u, 1, 1))
        upper = jnp.where(row == rows - 1, keep_north * north_ref[level:level + 1, :], pltpu.roll(v, rows - 1, 0))
        lower = jnp.where(row == 0, keep_south * south_ref[level:level + 1, :], pltpu.roll(v, 1, 0))
        base_ref[level] = zonal * (ahead - behind) + merid * (upper - lower)


def pack_edges(u_ref, v_ref, first_col, last_col, first_row, last_row):
    rows, width = u_ref.shape[1:]
    lane = lax.broadcasted_iota(jnp.int32, (rows, LANE), 1)
    first = jnp.zeros((rows, LANE), jnp.float32)
    last = jnp.zeros((rows, LANE), jnp.float32)
    for level in range(u_ref.shape[0]):
        first = jnp.where(lane == level, u_ref[level, :, 0:1], first)
        last = jnp.where(lane == level, u_ref[level, :, width - 1:width], last)
        first_row[level:level + 1, :] = v_ref[level, 0:1, :]
        last_row[level:level + 1, :] = v_ref[level, rows - 1:rows, :]
    first_col[...] = first
    last_col[...] = last


def pack_halo(source, low, high, units):
    rows = source.shape[1]
    for g in range(low.shape[0]):
        for l in range(units):
            low[g, 2 * l:2 * l + 2, :] = source[g * units + l, 0:2, :]
            high[g, 2 * l:2 * l + 2, :] = source[g * units + l, rows - 2:rows, :]


def own_coefs(zc_ref, mc_ref, cutoff_ref, mask_ref, own_ref, first_lat, unfiltered):
    rows = own_ref.shape[1]
    row = lax.broadcasted_iota(jnp.int32, own_ref.shape[1:], 0)
    zonal = jnp.zeros(own_ref.shape[1:], jnp.float32)
    merid = jnp.zeros(own_ref.shape[1:], jnp.float32)
    limit = jnp.zeros(own_ref.shape[1:], jnp.int32)
    for r in range(rows):
        zonal = jnp.where(row == r, zc_ref[r], zonal)
        merid = jnp.where(row == r, mc_ref[r], merid)
        filtered = mask_ref[first_lat + r]
        bound = filtered * cutoff_ref[first_lat + r] + (1 - filtered) * unfiltered
        limit = jnp.where(row == r, bound, limit)
    own_ref[0] = zonal
    own_ref[1] = merid
    own_ref[2] = limit.astype(jnp.float32)


def fused_kernel(
    bands, per_band, a_ref, zc_ref, mc_ref, cutoff_ref, mask_ref, u_ref, v_ref, w_far, p_ref, s_far, high_far, rest_far, rows_ref,
    u_out, v_out, w_out, p_out,
    d1, d2, ur, vr, ds1, ds2, us, vs, w_mid, p_mid, base, ratio, inv,
    x1, x2, wide, work, qwork, vwork, spec, own_ref, near, cols_send, cols_recv, rows_send, rows_recv, low, high,
    send_sems, recv_sems, edge_send, edge_recv, halo_send, halo_recv,
    w_ref, s_ref, high_ref, rest_ref, load_sems,
):
    count = bands * per_band
    band_me = lax.axis_index("lat")
    lon_me = lax.axis_index("lon")
    me = band_me * per_band + lon_me
    half = high_ref.shape[0]
    lat_rows = u_ref.shape[1]
    units = u_ref.shape[0] // per_band
    spread = units + 2
    mesh_id = pl.DeviceIdType.MESH
    is_first = band_me == 0
    is_last = band_me == bands - 1

    loads = [
        pltpu.make_async_copy(far, here, load_sems.at[n])
        for n, (far, here) in enumerate(((high_far, high_ref), (rest_far, rest_ref), (s_far, s_ref), (w_far, w_ref)))
    ]
    for load in loads:
        load.start()
    barrier = pltpu.get_barrier_semaphore()

    def greet(i, carry):
        other = (me + i) % count
        pl.semaphore_signal(barrier, inc=1, device_id=(other // per_band, other % per_band), device_id_type=mesh_id)
        return carry

    lax.fori_loop(1, count, greet, 0)
    own_coefs(zc_ref, mc_ref, cutoff_ref, mask_ref, own_ref, band_me * lat_rows, half * TILE)
    pack_halo(p_ref, low.at[0], high.at[0], units)
    pack_edges(u_ref, v_ref, cols_send.at[0], cols_send.at[1], rows_send.at[0], rows_send.at[1])

    @pl.when(is_first)
    def _():
        near[0] = jnp.zeros(near.shape[1:], jnp.float32)
        for d in range(per_band):
            x1[d * spread + units] = jnp.zeros(x1.shape[1:], jnp.float32)
            x2[d * spread + units] = jnp.zeros(x2.shape[1:], jnp.float32)

    @pl.when(is_last)
    def _():
        near[1] = jnp.zeros(near.shape[1:], jnp.float32)
        for d in range(per_band):
            x1[d * spread + units + 1] = jnp.zeros(x1.shape[1:], jnp.float32)
            x2[d * spread + units + 1] = jnp.zeros(x2.shape[1:], jnp.float32)

    pl.semaphore_wait(barrier, count - 1)

    def scatter(source, target, sem, stride):
        def one(i, carry):
            g = (lon_me + i) % per_band
            pltpu.make_async_remote_copy(
                src_ref=source.at[pl.ds(g * units, units)], dst_ref=target.at[pl.ds(lon_me * stride, units)],
                send_sem=send_sems.at[sem], recv_sem=recv_sems.at[sem],
                device_id=(band_me, g), device_id_type=mesh_id,
            ).start()
            return carry

        lax.fori_loop(1, per_band, one, 0)
        for l in range(units):
            target[lon_me * stride + l] = source[lon_me * units + l]

    def gathered(target, sem):
        block = target.at[pl.ds(0, (per_band - 1) * units)]
        pltpu.make_async_copy(block, block, recv_sems.at[sem]).wait()

    def sent(source, sem):
        block = source.at[pl.ds(0, (per_band - 1) * units)]
        pltpu.make_async_copy(block, block, send_sems.at[sem]).wait()

    def spread_halo(target, phase):
        def one(source, slot, sem, other):
            def step(i, carry):
                g = (lon_me + i) % per_band
                pltpu.make_async_remote_copy(
                    src_ref=source.at[g], dst_ref=target.at[lon_me * spread + slot],
                    send_sem=halo_send.at[sem], recv_sem=halo_recv.at[sem],
                    device_id=(other, g), device_id_type=mesh_id,
                ).start()
                return carry

            lax.fori_loop(0, per_band, step, 0)

        @pl.when(jnp.logical_not(is_first))
        def _():
            one(low.at[phase], units + 1, 2 * phase, band_me - 1)

        @pl.when(jnp.logical_not(is_last))
        def _():
            one(high.at[phase], units, 2 * phase + 1, band_me + 1)

    def halo_wait(phase, sems, upward):
        block = low.at[phase]

        @pl.when(jnp.logical_not(is_first))
        def _():
            pltpu.make_async_copy(block, block, sems.at[2 * phase + (0 if upward else 1)]).wait()

        @pl.when(jnp.logical_not(is_last))
        def _():
            pltpu.make_async_copy(block, block, sems.at[2 * phase + (1 if upward else 0)]).wait()

    def coef_copy(step, side):
        return pltpu.make_async_remote_copy(
            src_ref=own_ref, dst_ref=near.at[side], send_sem=edge_send.at[4 + side], recv_sem=edge_recv.at[4 + side],
            device_id=((band_me + bands + step) % bands, lon_me), device_id_type=mesh_id,
        )

    @pl.when(jnp.logical_not(is_first))
    def _():
        coef_copy(-1, 1).start()

    @pl.when(jnp.logical_not(is_last))
    def _():
        coef_copy(1, 0).start()

    scatter(p_ref, x1, 0, spread)
    spread_halo(x1, 0)

    edge_copies = []
    for side, step in ((0, -1), (1, 1)):
        edge_copies.append(pltpu.make_async_remote_copy(
            src_ref=cols_send.at[side], dst_ref=cols_recv.at[side], send_sem=edge_send.at[side], recv_sem=edge_recv.at[side],
            device_id=(band_me, (lon_me + per_band + step) % per_band), device_id_type=mesh_id,
        ))
        edge_copies.append(pltpu.make_async_remote_copy(
            src_ref=rows_send.at[side], dst_ref=rows_recv.at[side], send_sem=edge_send.at[2 + side], recv_sem=edge_recv.at[2 + side],
            device_id=((band_me + bands + step) % bands, lon_me), device_id_type=mesh_id,
        ))
    for copy in edge_copies:
        copy.start()

    @pl.when(jnp.logical_not(is_first))
    def _():
        coef_copy(1, 0).wait_recv()

    @pl.when(jnp.logical_not(is_last))
    def _():
        coef_copy(-1, 1).wait_recv()

    for load in loads:
        load.wait()
    gathered(x1, 0)
    halo_wait(0, halo_recv, False)
    to_spectrum(x1, high_ref, rest_ref, wide, spec, spread, per_band, False)
    for t in range(half):
        _, _, d_parts = spectral_terms(spec, t, units, rows_ref, own_ref, near)
        d_part = jnp.concatenate(d_parts, axis=0)
        work[t] = three_products(d_part, high_ref[t], rest_ref[t], True).reshape(work.shape[1:])

    def first_back(unit, carry):
        put_blocks(ds1, circle_blocks(work, unit), unit, units)
        return carry

    lax.fori_loop(0, units, first_back, 0)
    scatter(ds1, d1, 1, units)

    factor_columns(a_ref, s_ref, ratio, inv)
    for copy in edge_copies:
        copy.wait_recv()
    base_divergence(
        u_ref, v_ref, own_ref, cols_recv.at[1], cols_recv.at[0], rows_recv.at[1], rows_recv.at[0], base,
        is_first, is_last,
    )
    gathered(d1, 1)
    solve_columns(a_ref, s_ref, w_ref, p_ref, base, d1, ratio, inv, w_mid, p_mid)
    scatter(p_mid, x2, 2, spread)
    pack_halo(p_mid, low.at[1], high.at[1], units)
    spread_halo(x2, 1)
    gathered(x2, 2)
    halo_wait(1, halo_recv, False)
    to_spectrum(x2, high_ref, rest_ref, wide, spec, spread, per_band, True)
    lats = units * lat_rows
    for t in range(half):
        smooth, v_parts, d_parts = spectral_terms(spec, t, units, rows_ref, own_ref, near)
        value = three_products(jnp.concatenate(d_parts + smooth + v_parts, axis=0), high_ref[t], rest_ref[t], True)
        work[t] = value[:lats].reshape(work.shape[1:])
        qwork[t] = value[lats:2 * lats].reshape(work.shape[1:])
        vwork[t] = value[2 * lats:].reshape(work.shape[1:])

    def second_back(band, carry):
        put_blocks(ds2, circle_blocks(work, band), band, units)
        return carry

    lax.fori_loop(0, units, second_back, 0)
    scatter(ds2, d2, 3, units)

    def winds_back(band, carry):
        put_blocks(vs, circle_blocks(vwork, band), band, units)
        zonal = own_ref[0, :, 0:1]
        moved = circle_diff(circle_blocks(qwork, band))
        put_blocks(us, [-zonal * x for x in moved], band, units)
        return carry

    lax.fori_loop(0, units, winds_back, 0)
    scatter(us, ur, 4, units)
    scatter(vs, vr, 5, units)
    gathered(d2, 3)
    solve_columns(a_ref, s_ref, w_mid, p_mid, base, d2, ratio, inv, w_out, p_out)
    gathered(ur, 4)
    u_out[...] = u_ref[...] + ur[...]
    gathered(vr, 5)
    v_out[...] = v_ref[...] + vr[...]
    for source, sem in ((p_ref, 0), (ds1, 1), (p_mid, 2), (ds2, 3), (us, 4), (vs, 5)):
        sent(source, sem)
    for phase in range(2):
        halo_wait(phase, halo_send, True)
    for copy in edge_copies:
        copy.wait_send()

    @pl.when(jnp.logical_not(is_first))
    def _():
        coef_copy(-1, 1).wait_send()

    @pl.when(jnp.logical_not(is_last))
    def _():
        coef_copy(1, 0).wait_send()


def deliver_kernel(*refs):
    count = (len(refs) - 1) // 2
    sems = refs[-1]
    copies = [pltpu.make_async_copy(refs[n], refs[count + n], sems.at[n]) for n in range(count)]
    for copy in copies:
        copy.start()
    for copy in copies:
        copy.wait()


def deliver(arrays):
    count = len(arrays)
    return pl.pallas_call(
        deliver_kernel,
        out_shape=tuple(jax.ShapeDtypeStruct(a.shape, a.dtype) for a in arrays),
        in_specs=[pl.BlockSpec(memory_space=pltpu.VMEM)] * count,
        out_specs=(pl.BlockSpec(memory_space=pl.ANY),) * count,
        scratch_shapes=[pltpu.SemaphoreType.DMA((count,))],
        compiler_params=pltpu.CompilerParams(vmem_limit_bytes=FINISH_VMEM),
    )(*arrays)


def level_body(
    tables,
    zonal_wind,
    merid_wind,
    vertical_wind,
    pressure,
    zonal_coef,
    merid_coef,
    level_coef,
    sound_coef,
    cutoff,
    filter_mask,
):
    high, rest, rows = (jnp.asarray(t) for t in tables)
    half = high.shape[0]
    bands = lax.axis_size("lat")
    per_band = lax.axis_size("lon")
    levels, lat_rows, width = pressure.shape
    units = levels // per_band
    spread = units + 2
    vmem = pl.BlockSpec(memory_space=pltpu.VMEM)
    smem = pl.BlockSpec(memory_space=pltpu.SMEM)
    far = pl.BlockSpec(memory_space=pl.ANY)
    block = jax.ShapeDtypeStruct(pressure.shape, jnp.float32)

    def scratch(*shape):
        return pltpu.VMEM(shape, jnp.float32)

    field = scratch(*pressure.shape)
    arrivals = scratch(per_band * spread, lat_rows, width)
    waves = scratch(half, units, lat_rows, TILE)
    dma = pltpu.SemaphoreType.DMA
    results = pl.pallas_call(
        functools.partial(fused_kernel, bands, per_band),
        out_shape=(pltpu.VMEM(pressure.shape, jnp.float32),) * 4,
        in_specs=[smem] * 5 + [vmem] * 2 + [far, vmem, far, far, far, vmem],
        out_specs=(vmem,) * 4,
        scratch_shapes=[field] * 13 + [arrivals] * 2 + [scratch(half, spread, lat_rows, TILE)] + [waves] * 3 + [
            scratch(half, spread * lat_rows, TILE),
            scratch(3, lat_rows, LANE), scratch(2, 3, lat_rows, LANE),
            scratch(2, lat_rows, LANE), scratch(2, lat_rows, LANE),
            scratch(2, levels, width), scratch(2, levels, width),
            scratch(2, per_band, lat_rows, width), scratch(2, per_band, lat_rows, width),
            dma((6,)), dma((6,)), dma((6,)), dma((6,)), dma((4,)), dma((4,)),
            field, field, pltpu.VMEM(high.shape, high.dtype), pltpu.VMEM(rest.shape, rest.dtype), dma((4,)),
        ],
        compiler_params=pltpu.CompilerParams(collective_id=0, has_side_effects=True, vmem_limit_bytes=FUSED_VMEM),
    )(*[pltpu.with_memory_space_constraint(x, pltpu.HBM) for x in (
        level_coef, zonal_coef, merid_coef, cutoff, filter_mask,
        zonal_wind, merid_wind, vertical_wind, pressure, sound_coef, high, rest, rows,
    )])
    return deliver(results)


def body(tables, *arrays):
    pressure = arrays[3]
    per_band = lax.axis_size("lon")
    levels, lat_rows, width = pressure.shape
    fits = lat_rows == 8 and levels == 4 * per_band and levels <= LANE and width % LANE == 0
    if fits:
        return level_body(tables, *arrays)
    return wide_body(*arrays)


def solution(mesh):
    in_specs = (
        P(None, "lat", "lon"),
        P(None, "lat", "lon"),
        P(None, "lat", "lon"),
        P(None, "lat", "lon"),
        P("lat"),
        P("lat"),
        P(),
        P(None, "lat", "lon"),
        P(),
        P(),
    )
    out_specs = (
        P(None, "lat", "lon"),
        P(None, "lat", "lon"),
        P(None, "lat", "lon"),
        P(None, "lat", "lon"),
    )

    def whole(*arrays):
        tables = circle_tables(arrays[0].shape[2])
        step = jax.shard_map(functools.partial(body, tables), mesh=mesh, in_specs=in_specs, out_specs=out_specs, check_vma=False)
        return step(*arrays)

    return whole
```

profile of v0, /device:TPU:0, one launch (start us, length us, event | category | flops | bytes accessed | tf_op | source)
XLA Modules:
  0.0 38.9 jit_solution(1816675261918611733)
XLA Ops:
  0.6 37.3 %shard_map.156 = (f32[32,8,256]{2,1,0:T(8,128)S(1)}, f32[32,8,256]{2,1,0:T(8,128)S(1)}, f32[32,8,256]{2,1,0:T(8,128)S(1)}, f32[32,8,256]{2,1,0:T(8,128)S(1)}) custom-call(f32[32]{0:T(128)} %a_ref.1, f32[8]{0:T(128)} %zc_ref.1, f32[8]{0:T(128)} %mc_ref.1, s32[32]{0:T(128)} %cutoff_ref.1, s32[32]{0:T(128)} %mask_ref.1, f32[32,8,256]{2,1,0:T(8,128)} %u_ref.1, ...), custom_call_target="tpu_custom_call" | custom-call | tf_op jit(solution)/shard_map/pallas_call | solution.py:713
  37.9 1.0 %shard_map.157 = (f32[32,8,256]{2,1,0:T(8,128)}, f32[32,8,256]{2,1,0:T(8,128)}, f32[32,8,256]{2,1,0:T(8,128)}, f32[32,8,256]{2,1,0:T(8,128)}) custom-call(f32[32,8,256]{2,1,0:T(8,128)S(1)} %get-tuple-element.8.refs_0_, f32[32,8,256]{2,1,0:T(8,128)S(1)} %get-tuple-element.9.refs_1_, f32[32,8,256]{2,1,0:T(8,128)S(1)} %get-tuple-element.10.refs_2_, ...), custom_call_target="tpu_custom_call" | custom-call | tf_op jit(solution)/shard_map/pallas_call | solution.py:671
where the time goes:
time: 39.1 us; the launch traced here: 38.9 us
  Pallas kernels  38.3 us (98%)
  between operations  0.64 us (2%)
    pallas_call x1, Pallas kernels, level_body(): pl.pallas_call(functools.partial(fused_kernel, bands, per_band), out_shap...  37.3 us
    pallas_call x1, Pallas kernels, deliver(): pl.pallas_call(deliver_kernel, out_shape=tuple((jax.ShapeDtypeStruct(a.sh...  1 us

commit v1 on v0

v1 whole, which is shorter than its diff:
```python
import functools
import math

import ml_dtypes
import numpy as np
import jax
import jax.numpy as jnp
from jax import lax
from jax.experimental import pallas as pl
from jax.experimental.pallas import tpu as pltpu
from jax.sharding import PartitionSpec as P

SUBSTEPS = 2
FUSED_VMEM = 40 * 2 ** 20
FINISH_VMEM = 4 * 2 ** 20


def extended(block, sides, width):
    for axis, dim in sides:
        count = lax.axis_size(axis)
        forward = [(i, i + 1) for i in range(count - 1)]
        forward.append((count - 1, 0))
        backward = [(target, source) for source, target in forward]
        low = lax.ppermute(
            lax.slice_in_dim(block, block.shape[dim] - width, None, axis=dim), axis, forward
        )
        high = lax.ppermute(lax.slice_in_dim(block, 0, width, axis=dim), axis, backward)
        block = jnp.concatenate([low, block, high], axis=dim)
    return block


def rim_fix(padded, lat_dim):
    band_index = lax.axis_index("lat")
    bands = lax.axis_size("lat")
    extent = padded.shape[lat_dim]
    position = lax.broadcasted_iota(jnp.int32, padded.shape, lat_dim)
    first_edge = jnp.logical_and(position == 0, band_index == 0)
    final_edge = jnp.logical_and(position == extent - 1, band_index == bands - 1)
    return jnp.where(jnp.logical_or(first_edge, final_edge), 0.0, padded)


def dft_tables(length):
    half_len = length // 2
    sample = lax.broadcasted_iota(jnp.int32, (length, length), 0)
    column = lax.broadcasted_iota(jnp.int32, (length, length), 1)
    is_cosine = column <= half_len
    wavenum = jnp.where(is_cosine, column, column - half_len)
    phase = sample * wavenum % length
    angle = 2.0 * math.pi / length * phase.astype(jnp.float32)
    forward = jnp.where(is_cosine, jnp.cos(angle), jnp.sin(angle))
    single = jnp.logical_and(is_cosine, jnp.logical_or(wavenum == 0, wavenum == half_len))
    weight = jnp.where(single, 1.0, 2.0) / length
    inverse = jnp.transpose(forward * weight)
    wave_row = wavenum[0].astype(jnp.float32)
    return (forward, inverse, wave_row)


def damping(wave_row, limits):
    bound_col = limits[:, None]
    ratio = bound_col / jnp.maximum(wave_row[None, :], 1.0)
    return jnp.where(wave_row[None, :] > bound_col, ratio * ratio, 1.0)


def transform_band(block, limits, forward, inverse, wave_row):
    circles = lax.all_to_all(block, "lon", split_axis=1, concat_axis=3, tiled=True)
    spectra = jnp.einsum("vetj,jc->vetc", circles, forward, precision=lax.Precision.HIGHEST)
    scaled = spectra * damping(wave_row, limits)
    damped = jnp.einsum("vetc,cj->vetj", scaled, inverse, precision=lax.Precision.HIGHEST)
    return lax.all_to_all(damped, "lon", split_axis=3, concat_axis=1, tiled=True)


def filtered_increments(increments, own_flags, own_limits, forward, inverse, wave_row):
    flag_cols = own_flags[:, None]
    damped = transform_band(increments, own_limits, forward, inverse, wave_row)
    return jnp.where(flag_cols, damped, increments)


def column_solve(vertical_wind, pstar, level_coef, sound_coef):
    levels = vertical_wind.shape[0]
    zero_slab = jnp.zeros_like(vertical_wind[0])
    ratios = []
    values = []
    prev_ratio = zero_slab
    prev_value = zero_slab
    for level in range(levels):
        alpha = level_coef[level]
        below = alpha * sound_coef[level]
        if level + 1 < levels:
            above = alpha * sound_coef[level + 1]
            rhs = vertical_wind[level] - alpha * (pstar[level + 1] - pstar[level])
        else:
            above = zero_slab
            rhs = vertical_wind[level] + alpha * pstar[level]
        pivot = 1.0 + below + above + below * prev_ratio
        prev_ratio = -above / pivot
        prev_value = (rhs + below * prev_value) / pivot
        ratios.append(prev_ratio)
        values.append(prev_value)
    solved = [zero_slab] * levels
    upper_value = values[levels - 1]
    solved[levels - 1] = upper_value
    for level in range(levels - 2, -1, -1):
        upper_value = values[level] - ratios[level] * upper_value
        solved[level] = upper_value
    new_wind = jnp.stack(solved)
    wind_below = jnp.concatenate([zero_slab[None], new_wind[:-1]], axis=0)
    new_pressure = pstar - sound_coef * (new_wind - wind_below)
    return (new_wind, new_pressure)


def wide_body(
    zonal_wind,
    merid_wind,
    vertical_wind,
    pressure,
    zonal_coef,
    merid_coef,
    level_coef,
    sound_coef,
    cutoff,
    filter_mask,
):
    lat_rows = pressure.shape[1]
    start = lax.axis_index("lat") * lat_rows
    own_flags = lax.dynamic_slice_in_dim(filter_mask, start, lat_rows) > 0
    own_limits = lax.dynamic_slice_in_dim(cutoff, start, lat_rows).astype(jnp.float32)
    forward, inverse, wave_row = dft_tables(pressure.shape[2] * lax.axis_size("lon"))
    zonal_rows = zonal_coef[None, :, None]
    merid_rows = merid_coef[None, :, None]
    for step in range(SUBSTEPS):
        padded = extended(pressure, (("lat", 1), ("lon", 2)), 1)
        padded = rim_fix(padded, 1)
        zonal_step = -zonal_rows * (padded[:, 1:-1, 2:] - padded[:, 1:-1, :-2])
        merid_step = -merid_rows * (padded[:, 2:, 1:-1] - padded[:, :-2, 1:-1])
        increments = jnp.stack([zonal_step, merid_step])
        damped = filtered_increments(increments, own_flags, own_limits, forward, inverse, wave_row)
        winds = jnp.stack([zonal_wind, merid_wind]) + damped
        wind_pad = extended(winds, (("lat", 2), ("lon", 3)), 1)
        wind_pad = rim_fix(wind_pad, 2)
        diverge = zonal_rows * (wind_pad[0, :, 1:-1, 2:] - wind_pad[0, :, 1:-1, :-2])
        diverge = diverge + merid_rows * (wind_pad[1, :, 2:, 1:-1] - wind_pad[1, :, :-2, 1:-1])
        pstar = pressure - sound_coef * diverge
        vertical_wind, pressure = column_solve(vertical_wind, pstar, level_coef, sound_coef)
        zonal_wind = winds[0]
        merid_wind = winds[1]
    return (zonal_wind, merid_wind, vertical_wind, pressure)


LANE = 128
TILE = 2 * LANE


def circle_tables(length):
    blocks = length // LANE
    half = blocks // 2
    m = np.arange(LANE, dtype=np.float64)[:, None]
    c = np.arange(LANE)[None, :]
    angle = 2 * np.pi * ((m * c) % LANE) / LANE
    cos, sin = np.cos(angle) / np.sqrt(LANE), np.sin(angle) / np.sqrt(LANE)
    table = np.block([[cos, -sin], [sin, cos]])
    high = table.astype(ml_dtypes.bfloat16)
    rest = (table - high.astype(np.float64)).astype(ml_dtypes.bfloat16)
    rows = np.zeros((half + 1, 8, TILE), np.float32)
    for k1 in range(half + 1):
        k = k1 + blocks * c[0]
        waves = np.tile(np.minimum(k, length - k), 2)
        scale = (1.0 if k1 in (0, half) else 2.0) / blocks
        turn = 2 * np.pi * m[:, 0] * k1 / length
        rows[k1, 0] = waves
        rows[k1, 1] = 4.0 * np.sin(2 * np.pi * waves / length) ** 2
        rows[k1, 2] = np.where(np.arange(TILE) < LANE, scale, -scale)
        rows[k1, 3] = np.concatenate([np.cos(turn), np.sin(turn)])
    return np.stack([high, rest]), rows


def split_parts(value):
    high = value.astype(jnp.bfloat16)
    rest = (value - high.astype(jnp.float32)).astype(jnp.bfloat16)
    return high, rest


def three_products(value, table_ref):
    high, rest = split_parts(value)
    dims = (((1,), (0,)), ((), ()))
    rows = value.shape[0]
    table = table_ref[0]
    both = lax.dot_general(jnp.concatenate([high, rest], axis=0), table, dims, preferred_element_type=jnp.float32)
    corr = lax.dot_general(high, table_ref[1], dims, preferred_element_type=jnp.float32)
    return both[:rows] + (both[rows:] + corr)


def weighted(terms):
    total = None
    for coef, value in terms:
        if abs(coef) < 1e-12:
            continue
        if abs(abs(coef) - 1.0) < 1e-12:
            term = value
        else:
            term = abs(coef) * value
        if total is None:
            total = term if coef > 0 else -term
        else:
            total = total + term if coef > 0 else total - term
    return total


def coarse_forward(xs):
    count = len(xs)
    half = count // 2
    even = {b: xs[b] + xs[count - b] for b in range(1, half)}
    odd = {b: xs[b] - xs[count - b] for b in range(1, half)}
    real, imag = [], {}
    for k in range(half + 1):
        ends = xs[0] + xs[half] if k % 2 == 0 else xs[0] - xs[half]
        real.append(weighted([(1.0, ends)] + [(math.cos(2 * math.pi * b * k / count), even[b]) for b in range(1, half)]))
    for k in range(1, half):
        imag[k] = weighted([(-math.sin(2 * math.pi * b * k / count), odd[b]) for b in range(1, half)])
    pairs = [(real[0], real[half])] + [(real[k], imag[k]) for k in range(1, half)]
    return pairs


def coarse_inverse(pairs):
    half = len(pairs)
    count = 2 * half
    first, last = pairs[0]
    xs = [None] * count
    for b in range(half + 1):
        ends = first + last if b % 2 == 0 else first - last
        cos_part = weighted([(1.0, ends)] + [(math.cos(2 * math.pi * b * k / count), pairs[k][0]) for k in range(1, half)])
        if b in (0, half):
            xs[b] = cos_part
        else:
            sin_part = weighted([(-math.sin(2 * math.pi * b * k / count), pairs[k][1]) for k in range(1, half)])
            xs[b] = cos_part + sin_part
            xs[count - b] = cos_part - sin_part
    return xs


def whole_tiles(count):
    return -(-count // 16) * 16


def forward_fill(xs, rows_ref, work_ref, start):
    pairs = coarse_forward(xs)
    half = len(pairs)
    first, last = pairs[0]
    for t in range(half + 1):
        cos, sin = rows_ref[t, 3:4, :LANE], rows_ref[t, 3:4, LANE:]
        if t == 0:
            left, right = first, jnp.zeros_like(first)
        elif t == half:
            left, right = last * cos, -(last * sin)
        else:
            real, imag = pairs[t]
            left, right = real * cos + imag * sin, imag * cos - real * sin
        work_ref[start + 8 * t:start + 8 * t + 8, :LANE] = left
        work_ref[start + 8 * t:start + 8 * t + 8, LANE:] = right


def inverse_blocks(back_ref, rows_ref, start):
    half = rows_ref.shape[0] - 1
    pairs = []
    ends = []
    for t in range(half + 1):
        left = back_ref[start + 8 * t:start + 8 * t + 8, :LANE]
        right = back_ref[start + 8 * t:start + 8 * t + 8, LANE:]
        cos, sin = rows_ref[t, 3:4, :LANE], rows_ref[t, 3:4, LANE:]
        if t == 0:
            ends.append(left)
        elif t == half:
            ends.append(left * cos + right * sin)
        else:
            pairs.append((left * cos + right * sin, left * sin - right * cos))
    return coarse_inverse([tuple(ends)] + pairs)


def put_blocks(out_ref, xs, unit, units):
    split = out_ref.shape[2] // LANE
    for b, value in enumerate(xs):
        out_ref[(b // split) * units + unit, :, (b % split) * LANE:(b % split + 1) * LANE] = value


def circle_diff(xs):
    count = len(xs)
    lane = lax.broadcasted_iota(jnp.int32, xs[0].shape, 1)
    ahead = [pltpu.roll(x, LANE - 1, 1) for x in xs]
    behind = [pltpu.roll(x, 1, 1) for x in xs]
    out = []
    for b in range(count):
        nxt = jnp.where(lane == LANE - 1, ahead[(b + 1) % count], ahead[b])
        prv = jnp.where(lane == 0, behind[(b - 1) % count], behind[b])
        out.append(nxt - prv)
    return out


def border_tiles(edge_ref, xs, unit):
    count = len(xs)
    split = count // edge_ref.shape[0]
    lane = lax.broadcasted_iota(jnp.int32, xs[0].shape, 1)
    turned = [pltpu.roll(x, 2 * unit + 1, 1) for x in xs]
    for d in range(edge_ref.shape[0]):
        west, east = turned[(d * split - 1) % count], turned[(d * split + split) % count]
        kept = edge_ref[d] if unit else jnp.zeros_like(west)
        edge_ref[d] = jnp.where(lane == 2 * unit, west, jnp.where(lane == 2 * unit + 1, east, kept))


def filter_values(limit, wave, scale):
    quotient = limit / jnp.maximum(wave, 1.0)
    return jnp.where(wave > limit, quotient * quotient, 1.0) * scale


def filter_terms(rows_ref, own_ref, near_ref, filt_ref, side_ref):
    rows = own_ref.shape[1]
    zonal, merid, limit = own_ref[0, :, 0:1], own_ref[1, :, 0:1], own_ref[2, :, 0:1]
    for t in range(rows_ref.shape[0]):
        wave, sines, scale = rows_ref[t, 0:1, :], rows_ref[t, 1:2, :], rows_ref[t, 2:3, :]
        factor = filter_values(limit, wave, scale)
        filt_ref[t, 0] = factor
        filt_ref[t, 1] = merid * factor
        filt_ref[t, 2] = (zonal * zonal) * sines * factor
        south = near_ref[0, 1, rows - 1:rows, 0:1] * filter_values(near_ref[0, 2, rows - 1:rows, 0:1], wave, scale)
        north = near_ref[1, 1, 0:1, 0:1] * filter_values(near_ref[1, 2, 0:1, 0:1], wave, scale)
        side_ref[t, 0:1, :] = south
        side_ref[t, 1:2, :] = north


def merid_terms(spec_ref, unit, t, filt_ref, side_ref):
    tile = spec_ref.shape[1] // filt_ref.shape[0]
    units = spec_ref.shape[0] - 2
    own = spec_ref[unit, tile * t:tile * t + tile, :]
    row = lax.broadcasted_iota(jnp.int32, own.shape, 0)
    at = tile * t + 2 * unit
    below_far, below = spec_ref[units, at:at + 1, :], spec_ref[units, at + 1:at + 2, :]
    above, above_far = spec_ref[units + 1, at:at + 1, :], spec_ref[units + 1, at + 1:at + 2, :]
    upper = jnp.where(row == tile - 1, above, pltpu.roll(own, tile - 1, 0))
    lower = jnp.where(row == 0, below, pltpu.roll(own, 1, 0))
    mid = -filt_ref[t, 1] * (upper - lower)
    v_south = -side_ref[t, 0:1, :] * (own[0:1] - below_far)
    v_north = -side_ref[t, 1:2, :] * (above_far - own[tile - 1:tile])
    return own, row, mid, v_south, v_north


def factor_columns(a_ref, s_ref, ratio_ref, inv_ref):
    levels = s_ref.shape[0]
    prev = jnp.zeros(s_ref.shape[1:], jnp.float32)
    for level in range(levels):
        alpha = a_ref[level]
        below = alpha * s_ref[level]
        above = alpha * s_ref[level + 1] if level + 1 < levels else jnp.zeros_like(below)
        inv = 1.0 / (1.0 + below + above + below * prev)
        prev = -above * inv
        ratio_ref[level] = prev
        inv_ref[level] = inv


def solve_columns(a_ref, s_ref, w_ref, p_ref, parts, ratio_ref, inv_ref, w_out, p_out):
    levels = s_ref.shape[0]

    def star(level):
        total = parts[0][level]
        for part in parts[1:]:
            total = total + part[level]
        return p_ref[level] - s_ref[level] * total

    here = star(0)
    prev = jnp.zeros_like(here)
    for level in range(levels):
        alpha = a_ref[level]
        p_out[level] = here
        if level + 1 < levels:
            nxt = star(level + 1)
            rhs = w_ref[level] - alpha * (nxt - here)
        else:
            nxt = here
            rhs = w_ref[level] + alpha * here
        prev = (rhs + alpha * s_ref[level] * prev) * inv_ref[level]
        w_out[level] = prev
        here = nxt
    upper = w_out[levels - 1]
    for level in range(levels - 1, 0, -1):
        lower = w_out[level - 1] - ratio_ref[level - 1] * upper
        w_out[level - 1] = lower
        p_out[level] = p_out[level] - s_ref[level] * (upper - lower)
        upper = lower
    p_out[0] = p_out[0] - s_ref[0] * upper


def divergence(u, v, zonal, merid, west, east, south, north):
    rows, width = u.shape
    lane = lax.broadcasted_iota(jnp.int32, (rows, width), 1)
    row = lax.broadcasted_iota(jnp.int32, (rows, width), 0)
    ahead = jnp.where(lane == width - 1, east, pltpu.roll(u, width - 1, 1))
    behind = jnp.where(lane == 0, west, pltpu.roll(u, 1, 1))
    upper = jnp.where(row == rows - 1, north, pltpu.roll(v, rows - 1, 0))
    lower = jnp.where(row == 0, south, pltpu.roll(v, 1, 0))
    return zonal * (ahead - behind) + merid * (upper - lower)


def base_divergence(u_ref, v_ref, own_ref, west_ref, east_ref, south_ref, north_ref, base_ref, is_first, is_last):
    zonal, merid = own_ref[0, :, 0:1], own_ref[1, :, 0:1]
    keep_south = jnp.where(is_first, 0.0, 1.0)
    keep_north = jnp.where(is_last, 0.0, 1.0)
    west = west_ref[...]
    east = east_ref[...]
    for level in range(u_ref.shape[0]):
        base_ref[level] = divergence(
            u_ref[level], v_ref[level], zonal, merid, west[:, level:level + 1], east[:, level:level + 1],
            keep_south * south_ref[level:level + 1, :], keep_north * north_ref[level:level + 1, :],
        )


def added_divergence(ur, vr, own_ref, border_ref, rim_ref, base_ref, units):
    zonal, merid = own_ref[0, :, 0:1], own_ref[1, :, 0:1]
    for d in range(border_ref.shape[0]):
        border = border_ref[d]
        for l in range(units):
            level = d * units + l
            base_ref[level] = base_ref[level] + divergence(
                ur[level], vr[level], zonal, merid, border[:, 2 * l:2 * l + 1], border[:, 2 * l + 1:2 * l + 2],
                rim_ref[d, 2 * l:2 * l + 1, :], rim_ref[d, 2 * l + 1:2 * l + 2, :],
            )


def pack_edges(u_ref, v_ref, first_col, last_col, first_row, last_row):
    rows, width = u_ref.shape[1:]
    lane = lax.broadcasted_iota(jnp.int32, (rows, LANE), 1)
    first = jnp.zeros((rows, LANE), jnp.float32)
    last = jnp.zeros((rows, LANE), jnp.float32)
    for level in range(u_ref.shape[0]):
        first = jnp.where(lane == level, u_ref[level, :, 0:1], first)
        last = jnp.where(lane == level, u_ref[level, :, width - 1:width], last)
        first_row[level:level + 1, :] = v_ref[level, 0:1, :]
        last_row[level:level + 1, :] = v_ref[level, rows - 1:rows, :]
    first_col[...] = first
    last_col[...] = last


def pack_halo(source, low, high, units):
    rows = source.shape[1]
    for g in range(low.shape[0]):
        for l in range(units):
            low[g, 2 * l:2 * l + 2, :] = source[g * units + l, 0:2, :]
            high[g, 2 * l:2 * l + 2, :] = source[g * units + l, rows - 2:rows, :]


def own_coefs(zc_ref, mc_ref, cutoff_ref, mask_ref, own_ref, first_lat, unfiltered):
    rows = own_ref.shape[1]
    row = lax.broadcasted_iota(jnp.int32, own_ref.shape[1:], 0)
    zonal = jnp.zeros(own_ref.shape[1:], jnp.float32)
    merid = jnp.zeros(own_ref.shape[1:], jnp.float32)
    limit = jnp.zeros(own_ref.shape[1:], jnp.int32)
    for r in range(rows):
        zonal = jnp.where(row == r, zc_ref[r], zonal)
        merid = jnp.where(row == r, mc_ref[r], merid)
        filtered = mask_ref[first_lat + r]
        bound = filtered * cutoff_ref[first_lat + r] + (1 - filtered) * unfiltered
        limit = jnp.where(row == r, bound, limit)
    own_ref[0] = zonal
    own_ref[1] = merid
    own_ref[2] = limit.astype(jnp.float32)


def flipped(index, mask):
    bit = 1
    while bit <= mask:
        if mask & bit:
            index = index + bit * (1 - 2 * (index // bit % 2))
        bit *= 2
    return index


def partner_masks(count):
    return sorted(range(1, count), key=lambda mask: (-bin(mask // 2).count("1"), mask % 2, mask))


def fused_kernel(
    bands, per_band, a_far, zc_far, mc_far, cutoff_far, mask_far, u_far, v_far, w_far, p_far, s_far, table_far, rows_far,
    u_out, v_out, w_out, p_out,
    x1, x2, d1, ur, vr, ds1, us, vs, w_mid, p_mid, base, ratio, inv, u_ref, v_ref, w_ref, p_ref, s_ref,
    halo1, halo2, low, high, table_ref, rows_ref, spec, work, back, filt, sides,
    own_ref, near, cols_send, cols_recv, rows_send, rows_recv, border_send, border_recv, rim_send, rim_recv,
    a_ref, zc_ref, mc_ref, cutoff_ref, mask_ref,
    load_sems, send_sems, recv_sems, edge_send, edge_recv, halo_send, halo_recv, last_send, last_recv,
):
    band_me = lax.axis_index("lat")
    lon_me = lax.axis_index("lon")
    lat_rows = u_ref.shape[1]
    units = u_ref.shape[0] // per_band
    channels = rows_ref.shape[0]
    half = channels - 1
    per_unit = channels * lat_rows
    split = u_ref.shape[2] // LANE
    mesh_id = pl.DeviceIdType.MESH
    is_first = band_me == 0
    is_last = band_me == bands - 1
    not_first = jnp.logical_not(is_first)
    not_last = jnp.logical_not(is_last)
    masks = partner_masks(per_band)
    partners = [flipped(lon_me, mask) for mask in masks]

    pairs = (
        (p_far, p_ref), (zc_far, zc_ref), (mc_far, mc_ref), (cutoff_far, cutoff_ref), (mask_far, mask_ref), (a_far, a_ref),
        (rows_far, rows_ref), (u_far, u_ref), (v_far, v_ref), (table_far, table_ref), (s_far, s_ref), (w_far, w_ref),
    )
    loads = [pltpu.make_async_copy(far, here, load_sems.at[n]) for n, (far, here) in enumerate(pairs)]
    for load in loads:
        load.start()
    barrier = pltpu.get_barrier_semaphore()

    def greet(band, lon):
        pl.semaphore_signal(barrier, inc=1, device_id=(band, lon), device_id_type=mesh_id)

    for partner in partners:
        greet(band_me, partner)
    for there, step in ((not_first, -1), (not_last, 1)):
        @pl.when(there)
        def _():
            for other in partners + [lon_me]:
                greet(band_me + step, other)

    loads[0].wait()
    pack_halo(p_ref, low.at[0], high.at[0], units)
    expected = per_band - 1 + jnp.where(is_first, 0, per_band) + jnp.where(is_last, 0, per_band)
    pl.semaphore_wait(barrier, expected)

    def scatter(source, target, sem, unit):
        for g in partners:
            pltpu.make_async_remote_copy(
                src_ref=source.at[pl.ds(g * units + unit, 1)], dst_ref=target.at[pl.ds(lon_me * units + unit, 1)],
                send_sem=send_sems.at[sem], recv_sem=recv_sems.at[sem, unit],
                device_id=(band_me, g), device_id_type=mesh_id,
            ).start()
        target[lon_me * units + unit] = source[lon_me * units + unit]

    def gathered(target, sem, unit):
        block = target.at[pl.ds(0, per_band - 1)]
        pltpu.make_async_copy(block, block, recv_sems.at[sem, unit]).wait()

    def sent(source, sem):
        block = source.at[pl.ds(0, (per_band - 1) * units)]
        pltpu.make_async_copy(block, block, send_sems.at[sem]).wait()

    def spread_halo(target, phase):
        def one(source, slot, sem, other):
            for g in partners + [lon_me]:
                pltpu.make_async_remote_copy(
                    src_ref=source.at[g], dst_ref=target.at[slot, lon_me],
                    send_sem=halo_send.at[sem], recv_sem=halo_recv.at[sem],
                    device_id=(other, g), device_id_type=mesh_id,
                ).start()

        @pl.when(not_first)
        def _():
            one(low.at[phase], 1, 2 * phase, band_me - 1)

        @pl.when(not_last)
        def _():
            one(high.at[phase], 0, 2 * phase + 1, band_me + 1)

    def halo_wait(phase, sems, upward):
        block = low.at[phase]

        @pl.when(not_first)
        def _():
            pltpu.make_async_copy(block, block, sems.at[2 * phase + (0 if upward else 1)]).wait()

        @pl.when(not_last)
        def _():
            pltpu.make_async_copy(block, block, sems.at[2 * phase + (1 if upward else 0)]).wait()

    def coef_copy(step, side):
        return pltpu.make_async_remote_copy(
            src_ref=own_ref, dst_ref=near.at[side], send_sem=edge_send.at[4 + side], recv_sem=edge_recv.at[4 + side],
            device_id=((band_me + bands + step) % bands, lon_me), device_id_type=mesh_id,
        )

    spread_halo(halo1, 0)
    for unit in range(units):
        scatter(p_ref, x1, 0, unit)

    for load in loads[1:7]:
        load.wait()
    own_coefs(zc_ref, mc_ref, cutoff_ref, mask_ref, own_ref, band_me * lat_rows, half * TILE)

    @pl.when(not_first)
    def _():
        coef_copy(-1, 1).start()

    @pl.when(not_last)
    def _():
        coef_copy(1, 0).start()

    @pl.when(is_first)
    def _():
        near[0] = jnp.zeros(near.shape[1:], jnp.float32)
        for g in range(per_band):
            halo1[0, g] = jnp.zeros(halo1.shape[2:], jnp.float32)
            halo2[0, g] = jnp.zeros(halo2.shape[2:], jnp.float32)

    @pl.when(is_last)
    def _():
        near[1] = jnp.zeros(near.shape[1:], jnp.float32)
        for g in range(per_band):
            halo1[1, g] = jnp.zeros(halo1.shape[2:], jnp.float32)
            halo2[1, g] = jnp.zeros(halo2.shape[2:], jnp.float32)

    work[...] = jnp.zeros(work.shape, jnp.float32)
    for load in loads[7:9]:
        load.wait()
    pack_edges(u_ref, v_ref, cols_send.at[0], cols_send.at[1], rows_send.at[0], rows_send.at[1])
    edge_copies = []
    for side, step in ((0, -1), (1, 1)):
        edge_copies.append(pltpu.make_async_remote_copy(
            src_ref=cols_send.at[side], dst_ref=cols_recv.at[side], send_sem=edge_send.at[side], recv_sem=edge_recv.at[side],
            device_id=(band_me, (lon_me + per_band + step) % per_band), device_id_type=mesh_id,
        ))
    for copy in edge_copies:
        copy.start()

    def row_copy(step, side):
        return pltpu.make_async_remote_copy(
            src_ref=rows_send.at[side], dst_ref=rows_recv.at[side], send_sem=edge_send.at[2 + side], recv_sem=edge_recv.at[2 + side],
            device_id=((band_me + bands + step) % bands, lon_me), device_id_type=mesh_id,
        )

    @pl.when(not_first)
    def _():
        row_copy(-1, 0).start()

    @pl.when(not_last)
    def _():
        row_copy(1, 1).start()

    @pl.when(is_first)
    def _():
        rows_recv[1] = jnp.zeros(rows_recv.shape[1:], jnp.float32)

    @pl.when(is_last)
    def _():
        rows_recv[0] = jnp.zeros(rows_recv.shape[1:], jnp.float32)

    for load in loads[9:]:
        load.wait()
    factor_columns(a_ref, s_ref, ratio, inv)

    @pl.when(not_first)
    def _():
        coef_copy(1, 0).wait_recv()

    @pl.when(not_last)
    def _():
        coef_copy(-1, 1).wait_recv()

    filter_terms(rows_ref, own_ref, near, filt, sides)

    def circles(source, first, count, stride):
        return [
            [source[d * stride + first + n, :, h * LANE:(h + 1) * LANE] for d in range(per_band) for h in range(split)]
            for n in range(count)
        ]

    def forward(tiles, places, accumulate):
        for n, xs in enumerate(tiles):
            forward_fill(xs, rows_ref, work, n * per_unit)
        used = len(tiles) * per_unit
        value = three_products(work[0:whole_tiles(used), :], table_ref)
        for n, place in enumerate(places):
            part = value[n * per_unit:(n + 1) * per_unit]
            spec[place] = spec[place] + part if accumulate else part

    def halo_spectra(halo, phase, accumulate):
        halo_wait(phase, halo_recv, False)
        tiles = [
            [halo[slot, d, :, h * LANE:(h + 1) * LANE] for d in range(per_band) for h in range(split)] for slot in range(2)
        ]
        forward(tiles, [units, units + 1], accumulate)

    def inverse(count):
        back[0:whole_tiles(count * per_unit), :] = three_products(work[0:whole_tiles(count * per_unit), :], table_ref)

    halo_spectra(halo1, 0, False)
    for unit in range(units):
        gathered(x1, 0, unit)
        forward(circles(x1, unit, 1, units), [unit], False)
        for t in range(channels):
            own, row, mid, v_south, v_north = merid_terms(spec, unit, t, filt, sides)
            upper = jnp.where(row == lat_rows - 1, v_north, pltpu.roll(mid, lat_rows - 1, 0))
            lower = jnp.where(row == 0, v_south, pltpu.roll(mid, 1, 0))
            merid = own_ref[1, :, 0:1]
            work[lat_rows * t:lat_rows * (t + 1), :] = filt[t, 2] * own + merid * (upper - lower)
        inverse(1)
        put_blocks(ds1, inverse_blocks(back, rows_ref, 0), unit, units)
        scatter(ds1, d1, 1, unit)

    for copy in edge_copies:
        copy.wait_recv()

    @pl.when(not_first)
    def _():
        row_copy(1, 1).wait_recv()

    @pl.when(not_last)
    def _():
        row_copy(-1, 0).wait_recv()

    base_divergence(
        u_ref, v_ref, own_ref, cols_recv.at[1], cols_recv.at[0], rows_recv.at[1], rows_recv.at[0], base,
        is_first, is_last,
    )
    for unit in range(units):
        gathered(d1, 1, unit)
    solve_columns(a_ref, s_ref, w_ref, p_ref, (base, d1), ratio, inv, w_mid, p_mid)
    pack_halo(p_mid, low.at[1], high.at[1], units)
    spread_halo(halo2, 1)
    for unit in range(units):
        scatter(p_mid, x2, 2, unit)

    halo_spectra(halo2, 1, True)
    rim_at = 2 * per_unit
    for unit in range(units):
        gathered(x2, 2, unit)
        forward(circles(x2, unit, 1, units), [unit], True)
        for t in range(channels):
            own, row, mid, v_south, v_north = merid_terms(spec, unit, t, filt, sides)
            work[lat_rows * t:lat_rows * (t + 1), :] = filt[t, 0] * own
            work[per_unit + lat_rows * t:per_unit + lat_rows * (t + 1), :] = mid
            rim = rim_at + lat_rows * t + 2 * unit
            work[rim:rim + 1, :] = v_south
            work[rim + 1:rim + 2, :] = v_north
        inverse(3 if unit == units - 1 else 2)
        zonal = own_ref[0, :, 0:1]
        moved = [-zonal * x for x in circle_diff(inverse_blocks(back, rows_ref, 0))]
        put_blocks(us, moved, unit, units)
        border_tiles(border_send, moved, unit)
        scatter(us, ur, 3, unit)
        put_blocks(vs, inverse_blocks(back, rows_ref, per_unit), unit, units)
        scatter(vs, vr, 4, unit)
    rims = inverse_blocks(back, rows_ref, rim_at)
    for b, value in enumerate(rims):
        rim_send[b // split, :, (b % split) * LANE:(b % split + 1) * LANE] = value

    def last_copy(source, target, n, g):
        return pltpu.make_async_remote_copy(
            src_ref=source.at[pl.ds(g, 1)], dst_ref=target.at[pl.ds(lon_me, 1)], send_sem=last_send.at[n], recv_sem=last_recv.at[n],
            device_id=(band_me, g), device_id_type=mesh_id,
        )

    for n, (source, target) in enumerate(((border_send, border_recv), (rim_send, rim_recv))):
        for g in partners:
            last_copy(source, target, n, g).start()
        target[lon_me] = source[lon_me]

    for unit in range(units):
        gathered(ur, 3, unit)
        gathered(vr, 4, unit)
        for d in range(per_band):
            level = d * units + unit
            u_out[level] = u_ref[level] + ur[level]
            v_out[level] = v_ref[level] + vr[level]
    for n, target in enumerate((border_recv, rim_recv)):
        block = target.at[pl.ds(0, per_band - 1)]
        pltpu.make_async_copy(block, block, last_recv.at[n]).wait()
    added_divergence(ur, vr, own_ref, border_recv, rim_recv, base, units)
    solve_columns(a_ref, s_ref, w_mid, p_mid, (base,), ratio, inv, w_out, p_out)
    for source, sem in ((p_ref, 0), (ds1, 1), (p_mid, 2), (us, 3), (vs, 4)):
        sent(source, sem)
    for n, source in enumerate((border_send, rim_send)):
        block = source.at[pl.ds(0, per_band - 1)]
        pltpu.make_async_copy(block, block, last_send.at[n]).wait()
    for phase in range(2):
        halo_wait(phase, halo_send, True)
    for copy in edge_copies:
        copy.wait_send()

    @pl.when(not_first)
    def _():
        coef_copy(-1, 1).wait_send()
        row_copy(-1, 0).wait_send()

    @pl.when(not_last)
    def _():
        coef_copy(1, 0).wait_send()
        row_copy(1, 1).wait_send()


def deliver_kernel(*refs):
    count = (len(refs) - 1) // 2
    sems = refs[-1]
    copies = [pltpu.make_async_copy(refs[n], refs[count + n], sems.at[n]) for n in range(count)]
    for copy in copies:
        copy.start()
    for copy in copies:
        copy.wait()


def deliver(arrays):
    count = len(arrays)
    return pl.pallas_call(
        deliver_kernel,
        out_shape=tuple(jax.ShapeDtypeStruct(a.shape, a.dtype) for a in arrays),
        in_specs=[pl.BlockSpec(memory_space=pltpu.VMEM)] * count,
        out_specs=(pl.BlockSpec(memory_space=pl.ANY),) * count,
        scratch_shapes=[pltpu.SemaphoreType.DMA((count,))],
        compiler_params=pltpu.CompilerParams(vmem_limit_bytes=FINISH_VMEM),
    )(*arrays)


def level_body(
    tables,
    zonal_wind,
    merid_wind,
    vertical_wind,
    pressure,
    zonal_coef,
    merid_coef,
    level_coef,
    sound_coef,
    cutoff,
    filter_mask,
):
    table, rows = (jnp.asarray(t) for t in tables)
    channels = rows.shape[0]
    bands = lax.axis_size("lat")
    per_band = lax.axis_size("lon")
    levels, lat_rows, width = pressure.shape
    units = levels // per_band
    per_unit = channels * lat_rows
    vmem = pl.BlockSpec(memory_space=pltpu.VMEM)
    far = pl.BlockSpec(memory_space=pl.ANY)

    def scratch(*shape):
        return pltpu.VMEM(shape, jnp.float32)

    field = scratch(*pressure.shape)
    halo = scratch(2, per_band, lat_rows, width)
    spare = scratch(whole_tiles(3 * per_unit), TILE)
    dma = pltpu.SemaphoreType.DMA
    operands = (
        level_coef, zonal_coef, merid_coef, cutoff, filter_mask,
        zonal_wind, merid_wind, vertical_wind, pressure, sound_coef, table, rows,
    )
    results = pl.pallas_call(
        functools.partial(fused_kernel, bands, per_band),
        out_shape=(pltpu.VMEM(pressure.shape, jnp.float32),) * 4,
        in_specs=[far] * len(operands),
        out_specs=(vmem,) * 4,
        scratch_shapes=[field] * 18 + [halo] * 4 + [
            pltpu.VMEM(table.shape, table.dtype), scratch(*rows.shape),
            scratch(units + 2, per_unit, TILE), spare, spare,
            scratch(channels, 3, lat_rows, TILE), scratch(channels, 8, TILE),
            scratch(3, lat_rows, LANE), scratch(2, 3, lat_rows, LANE),
            scratch(2, lat_rows, LANE), scratch(2, lat_rows, LANE),
            scratch(2, levels, width), scratch(2, levels, width),
            scratch(per_band, lat_rows, LANE), scratch(per_band, lat_rows, LANE),
            scratch(per_band, lat_rows, width), scratch(per_band, lat_rows, width),
            pltpu.SMEM(level_coef.shape, jnp.float32), pltpu.SMEM(zonal_coef.shape, jnp.float32),
            pltpu.SMEM(merid_coef.shape, jnp.float32), pltpu.SMEM(cutoff.shape, jnp.int32),
            pltpu.SMEM(filter_mask.shape, jnp.int32),
            dma((len(operands),)), dma((5,)), dma((5, units)), dma((6,)), dma((6,)), dma((4,)), dma((4,)), dma((2,)), dma((2,)),
        ],
        compiler_params=pltpu.CompilerParams(collective_id=0, has_side_effects=True, vmem_limit_bytes=FUSED_VMEM),
    )(*[pltpu.with_memory_space_constraint(x, pltpu.HBM) for x in operands])
    return deliver(results)


def body(tables, *arrays):
    pressure = arrays[3]
    per_band = lax.axis_size("lon")
    levels, lat_rows, width = pressure.shape
    fits = lat_rows == 8 and levels == 4 * per_band and levels <= LANE and width % LANE == 0 and per_band & (per_band - 1) == 0
    if fits:
        return level_body(tables, *arrays)
    return wide_body(*arrays)


def solution(mesh):
    in_specs = (
        P(None, "lat", "lon"),
        P(None, "lat", "lon"),
        P(None, "lat", "lon"),
        P(None, "lat", "lon"),
        P("lat"),
        P("lat"),
        P(),
        P(None, "lat", "lon"),
        P(),
        P(),
    )
    out_specs = (
        P(None, "lat", "lon"),
        P(None, "lat", "lon"),
        P(None, "lat", "lon"),
        P(None, "lat", "lon"),
    )

    def whole(*arrays):
        tables = circle_tables(arrays[0].shape[2])
        step = jax.shard_map(functools.partial(body, tables), mesh=mesh, in_specs=in_specs, out_specs=out_specs, check_vma=False)
        return step(*arrays)

    return whole
```

time: 39.1 us -> 32.1 us (0.82)
  Pallas kernels: 38.3 us -> 31.3 us
    pallas_call x1, Pallas kernels: 37.3 us -> 30.3 us  [level_body(): pl.pallas_call(functools.partial(fused_kernel, bands, per_band), out_shap...]
where the time goes in v1:
time: 32.1 us; the launch traced here: 32 us
  Pallas kernels  31.3 us (98%)
  between operations  0.64 us (2%)
    pallas_call x1, Pallas kernels, level_body(): pl.pallas_call(functools.partial(fused_kernel, bands, per_band), out_shap...  30.3 us
    pallas_call x1, Pallas kernels, deliver(): pl.pallas_call(deliver_kernel, out_shape=tuple((jax.ShapeDtypeStruct(a.sh...  1 us

profile of v1, /device:TPU:0, one launch (start us, length us, event | category | flops | bytes accessed | tf_op | source)
XLA Modules:
  0.0 32.0 jit_solution(1994003778818461464)
XLA Ops:
  0.6 30.3 %shard_map.147 = (f32[32,8,256]{2,1,0:T(8,128)S(1)}, f32[32,8,256]{2,1,0:T(8,128)S(1)}, f32[32,8,256]{2,1,0:T(8,128)S(1)}, f32[32,8,256]{2,1,0:T(8,128)S(1)}) custom-call(f32[32]{0:T(128)} %a_far.1, f32[8]{0:T(128)} %zc_far.1, f32[8]{0:T(128)} %mc_far.1, s32[32]{0:T(128)} %cutoff_far.1, s32[32]{0:T(128)} %mask_far.1, f32[32,8,256]{2,1,0:T(8,128)} %u_far.1, ...), custom_call_target="tpu_custom_call" | custom-call | tf_op jit(solution)/shard_map/pallas_call | solution.py:843
  31.0 1.0 %shard_map.148 = (f32[32,8,256]{2,1,0:T(8,128)}, f32[32,8,256]{2,1,0:T(8,128)}, f32[32,8,256]{2,1,0:T(8,128)}, f32[32,8,256]{2,1,0:T(8,128)}) custom-call(f32[32,8,256]{2,1,0:T(8,128)S(1)} %get-tuple-element.8.refs_0_, f32[32,8,256]{2,1,0:T(8,128)S(1)} %get-tuple-element.9.refs_1_, f32[32,8,256]{2,1,0:T(8,128)S(1)} %get-tuple-element.10.refs_2_, ...), custom_call_target="tpu_custom_call" | custom-call | tf_op jit(solution)/shard_map/pallas_call | solution.py:799

commit v2 on v1

--- a/solution.py
+++ b/solution.py
@@ -294,6 +294,19 @@
     return out
 
 
+def border_rows(edge_ref, send_ref):
+    for d in range(edge_ref.shape[0]):
+        send_ref[d] = jnp.sum(pltpu.roll(edge_ref[d], 0, 1, stride=8, stride_axis=0), axis=0, keepdims=True)
+
+
+def border_columns(row):
+    value = jnp.broadcast_to(row, (8, LANE))
+    place = lax.broadcasted_iota(jnp.int32, (8, LANE), 0)
+    for bit in (1, 2, 4):
+        value = jnp.where(place // bit % 2 == 1, pltpu.roll(value, LANE - 8 * bit, 1), value)
+    return value
+
+
 def border_tiles(edge_ref, xs, unit):
     count = len(xs)
     split = count // edge_ref.shape[0]
@@ -325,14 +338,12 @@
         side_ref[t, 1:2, :] = north
 
 
-def merid_terms(spec_ref, unit, t, filt_ref, side_ref):
+def merid_terms(spec_ref, unit, t, filt_ref, side_ref, south_ref, north_ref, at):
     tile = spec_ref.shape[1] // filt_ref.shape[0]
-    units = spec_ref.shape[0] - 2
     own = spec_ref[unit, tile * t:tile * t + tile, :]
     row = lax.broadcasted_iota(jnp.int32, own.shape, 0)
-    at = tile * t + 2 * unit
-    below_far, below = spec_ref[units, at:at + 1, :], spec_ref[units, at + 1:at + 2, :]
-    above, above_far = spec_ref[units + 1, at:at + 1, :], spec_ref[units + 1, at + 1:at + 2, :]
+    below_far, below = south_ref[at:at + 1, :], south_ref[at + 1:at + 2, :]
+    above, above_far = north_ref[at:at + 1, :], north_ref[at + 1:at + 2, :]
     upper = jnp.where(row == tile - 1, above, pltpu.roll(own, tile - 1, 0))
     lower = jnp.where(row == 0, below, pltpu.roll(own, 1, 0))
     mid = -filt_ref[t, 1] * (upper - lower)
@@ -410,16 +421,34 @@
         )
 
 
-def added_divergence(ur, vr, own_ref, border_ref, rim_ref, base_ref, units):
+def added_divergence(ur, vr, own_ref, base_ref, levels):
     zonal, merid = own_ref[0, :, 0:1], own_ref[1, :, 0:1]
+    for level in levels:
+        base_ref[level] = base_ref[level] + divergence(ur[level], vr[level], zonal, merid, 0.0, 0.0, 0.0, 0.0)
+
+
+def added_borders(own_ref, border_ref, base_ref, units):
+    zonal = own_ref[0, :, 0:1]
+    width = base_ref.shape[2]
+    lane = lax.broadcasted_iota(jnp.int32, (8, LANE), 1)
     for d in range(border_ref.shape[0]):
-        border = border_ref[d]
+        border = border_columns(border_ref[d])
         for l in range(units):
             level = d * units + l
-            base_ref[level] = base_ref[level] + divergence(
-                ur[level], vr[level], zonal, merid, border[:, 2 * l:2 * l + 1], border[:, 2 * l + 1:2 * l + 2],
-                rim_ref[d, 2 * l:2 * l + 1, :], rim_ref[d, 2 * l + 1:2 * l + 2, :],
-            )
+            west = jnp.where(lane == 0, zonal * border[:, 2 * l:2 * l + 1], 0.0)
+            east = jnp.where(lane == LANE - 1, zonal * border[:, 2 * l + 1:2 * l + 2], 0.0)
+            base_ref[level, :, :LANE] = base_ref[level, :, :LANE] - west
+            base_ref[level, :, width - LANE:] = base_ref[level, :, width - LANE:] + east
+
+
+def added_rims(own_ref, rim_ref, base_ref, units):
+    merid = own_ref[1, :, 0:1]
+    rows = base_ref.shape[1]
+    for d in range(rim_ref.shape[0]):
+        for l in range(units):
+            level = d * units + l
+            base_ref[level, 0:1, :] = base_ref[level, 0:1, :] - merid[0:1] * rim_ref[d, 2 * l:2 * l + 1, :]
+            base_ref[level, rows - 1:rows, :] = base_ref[level, rows - 1:rows, :] + merid[rows - 1:rows] * rim_ref[d, 2 * l + 1:2 * l + 2, :]
 
 
 def pack_edges(u_ref, v_ref, first_col, last_col, first_row, last_row):
@@ -478,10 +507,10 @@
     bands, per_band, a_far, zc_far, mc_far, cutoff_far, mask_far, u_far, v_far, w_far, p_far, s_far, table_far, rows_far,
     u_out, v_out, w_out, p_out,
     x1, x2, d1, ur, vr, ds1, us, vs, w_mid, p_mid, base, ratio, inv, u_ref, v_ref, w_ref, p_ref, s_ref,
-    halo1, halo2, low, high, table_ref, rows_ref, spec, work, back, filt, sides,
-    own_ref, near, cols_send, cols_recv, rows_send, rows_recv, border_send, border_recv, rim_send, rim_recv,
+    halo1, low, high, chain_send, chain_recv, table_ref, rows_ref, spec, work, back, filt, sides,
+    own_ref, near, cols_send, cols_recv, rows_send, rows_recv, border_tile, border_send, border_recv, rim_send, rim_recv,
     a_ref, zc_ref, mc_ref, cutoff_ref, mask_ref,
-    load_sems, send_sems, recv_sems, edge_send, edge_recv, halo_send, halo_recv, last_send, last_recv,
+    load_sems, send_sems, recv_sems, edge_send, edge_recv, halo_send, halo_recv, last_send, last_recv, chain_out, chain_in,
 ):
     band_me = lax.axis_index("lat")
     lon_me = lax.axis_index("lon")
@@ -520,7 +549,7 @@
                 greet(band_me + step, other)
 
     loads[0].wait()
-    pack_halo(p_ref, low.at[0], high.at[0], units)
+    pack_halo(p_ref, low, high, units)
     expected = per_band - 1 + jnp.where(is_first, 0, per_band) + jnp.where(is_last, 0, per_band)
     pl.semaphore_wait(barrier, expected)
 
@@ -541,7 +570,7 @@
         block = source.at[pl.ds(0, (per_band - 1) * units)]
         pltpu.make_async_copy(block, block, send_sems.at[sem]).wait()
 
-    def spread_halo(target, phase):
+    def spread_halo(target):
         def one(source, slot, sem, other):
             for g in partners + [lon_me]:
                 pltpu.make_async_remote_copy(
@@ -552,22 +581,27 @@
 
         @pl.when(not_first)
         def _():
-            one(low.at[phase], 1, 2 * phase, band_me - 1)
+            one(low, 1, 0, band_me - 1)
 
         @pl.when(not_last)
         def _():
-            one(high.at[phase], 0, 2 * phase + 1, band_me + 1)
-
-    def halo_wait(phase, sems, upward):
-        block = low.at[phase]
-
+            one(high, 0, 1, band_me + 1)
+
+    def halo_wait(sems, upward):
         @pl.when(not_first)
         def _():
-            pltpu.make_async_copy(block, block, sems.at[2 * phase + (0 if upward else 1)]).wait()
+            pltpu.make_async_copy(low, low, sems.at[0 if upward else 1]).wait()
 
         @pl.when(not_last)
         def _():
-            pltpu.make_async_copy(block, block, sems.at[2 * phase + (1 if upward else 0)]).wait()
+            pltpu.make_async_copy(low, low, sems.at[1 if upward else 0]).wait()
+
+    def chain_copy(unit, side):
+        return pltpu.make_async_remote_copy(
+            src_ref=chain_send.at[side, unit], dst_ref=chain_recv.at[side, unit],
+            send_sem=chain_out.at[side], recv_sem=chain_in.at[side, unit],
+            device_id=((band_me + bands + 1 - 2 * side) % bands, lon_me), device_id_type=mesh_id,
+        )
 
     def coef_copy(step, side):
         return pltpu.make_async_remote_copy(
@@ -575,7 +609,7 @@
             device_id=((band_me + bands + step) % bands, lon_me), device_id_type=mesh_id,
         )
 
-    spread_halo(halo1, 0)
+    spread_halo(halo1)
     for unit in range(units):
         scatter(p_ref, x1, 0, unit)
 
@@ -594,16 +628,16 @@
     @pl.when(is_first)
     def _():
         near[0] = jnp.zeros(near.shape[1:], jnp.float32)
+        chain_recv[0] = jnp.zeros(chain_recv.shape[1:], jnp.float32)
         for g in range(per_band):
             halo1[0, g] = jnp.zeros(halo1.shape[2:], jnp.float32)
-            halo2[0, g] = jnp.zeros(halo2.shape[2:], jnp.float32)
 
     @pl.when(is_last)
     def _():
         near[1] = jnp.zeros(near.shape[1:], jnp.float32)
+        chain_recv[1] = jnp.zeros(chain_recv.shape[1:], jnp.float32)
         for g in range(per_band):
             halo1[1, g] = jnp.zeros(halo1.shape[2:], jnp.float32)
-            halo2[1, g] = jnp.zeros(halo2.shape[2:], jnp.float32)
 
     work[...] = jnp.zeros(work.shape, jnp.float32)
     for load in loads[7:9]:
@@ -669,22 +703,19 @@
             part = value[n * per_unit:(n + 1) * per_unit]
             spec[place] = spec[place] + part if accumulate else part
 
-    def halo_spectra(halo, phase, accumulate):
-        halo_wait(phase, halo_recv, False)
-        tiles = [
-            [halo[slot, d, :, h * LANE:(h + 1) * LANE] for d in range(per_band) for h in range(split)] for slot in range(2)
-        ]
-        forward(tiles, [units, units + 1], accumulate)
-
     def inverse(count):
         back[0:whole_tiles(count * per_unit), :] = three_products(work[0:whole_tiles(count * per_unit), :], table_ref)
 
-    halo_spectra(halo1, 0, False)
+    halo_wait(halo_recv, False)
+    forward([
+        [halo1[slot, d, :, h * LANE:(h + 1) * LANE] for d in range(per_band) for h in range(split)] for slot in range(2)
+    ], [units, units + 1], False)
     for unit in range(units):
         gathered(x1, 0, unit)
         forward(circles(x1, unit, 1, units), [unit], False)
         for t in range(channels):
-            own, row, mid, v_south, v_north = merid_terms(spec, unit, t, filt, sides)
+            at = lat_rows * t + 2 * unit
+            own, row, mid, v_south, v_north = merid_terms(spec, unit, t, filt, sides, spec.at[units], spec.at[units + 1], at)
             upper = jnp.where(row == lat_rows - 1, v_north, pltpu.roll(mid, lat_rows - 1, 0))
             lower = jnp.where(row == 0, v_south, pltpu.roll(mid, 1, 0))
             merid = own_ref[1, :, 0:1]
@@ -711,34 +742,35 @@
     for unit in range(units):
         gathered(d1, 1, unit)
     solve_columns(a_ref, s_ref, w_ref, p_ref, (base, d1), ratio, inv, w_mid, p_mid)
-    pack_halo(p_mid, low.at[1], high.at[1], units)
-    spread_halo(halo2, 1)
     for unit in range(units):
         scatter(p_mid, x2, 2, unit)
 
-    halo_spectra(halo2, 1, True)
-    rim_at = 2 * per_unit
+    zonal = own_ref[0, :, 0:1]
     for unit in range(units):
         gathered(x2, 2, unit)
         forward(circles(x2, unit, 1, units), [unit], True)
         for t in range(channels):
-            own, row, mid, v_south, v_north = merid_terms(spec, unit, t, filt, sides)
-            work[lat_rows * t:lat_rows * (t + 1), :] = filt[t, 0] * own
-            work[per_unit + lat_rows * t:per_unit + lat_rows * (t + 1), :] = mid
-            rim = rim_at + lat_rows * t + 2 * unit
-            work[rim:rim + 1, :] = v_south
-            work[rim + 1:rim + 2, :] = v_north
-        inverse(3 if unit == units - 1 else 2)
-        zonal = own_ref[0, :, 0:1]
+            at = lat_rows * t
+            chain_send[0, unit, 2 * t:2 * t + 2, :] = spec[unit, at + lat_rows - 2:at + lat_rows, :]
+            chain_send[1, unit, 2 * t:2 * t + 2, :] = spec[unit, at:at + 2, :]
+
+        @pl.when(not_last)
+        def _():
+            chain_copy(unit, 0).start()
+
+        @pl.when(not_first)
+        def _():
+            chain_copy(unit, 1).start()
+
+        for t in range(channels):
+            at = lat_rows * t
+            work[at:at + lat_rows, :] = filt[t, 0] * spec[unit, at:at + lat_rows, :]
+        inverse(1)
         moved = [-zonal * x for x in circle_diff(inverse_blocks(back, rows_ref, 0))]
         put_blocks(us, moved, unit, units)
-        border_tiles(border_send, moved, unit)
         scatter(us, ur, 3, unit)
-        put_blocks(vs, inverse_blocks(back, rows_ref, per_unit), unit, units)
-        scatter(vs, vr, 4, unit)
-    rims = inverse_blocks(back, rows_ref, rim_at)
-    for b, value in enumerate(rims):
-        rim_send[b // split, :, (b % split) * LANE:(b % split + 1) * LANE] = value
+        border_tiles(border_tile, moved, unit)
+    border_rows(border_tile, border_send)
 
     def last_copy(source, target, n, g):
         return pltpu.make_async_remote_copy(
@@ -746,40 +778,76 @@
             device_id=(band_me, g), device_id_type=mesh_id,
         )
 
-    for n, (source, target) in enumerate(((border_send, border_recv), (rim_send, rim_recv))):
+    def last_scatter(source, target, n):
         for g in partners:
             last_copy(source, target, n, g).start()
         target[lon_me] = source[lon_me]
 
+    last_scatter(border_send, border_recv, 0)
+    rim_at = per_unit
+    for unit in range(units):
+        @pl.when(not_first)
+        def _():
+            chain_copy(unit, 0).wait_recv()
+
+        @pl.when(not_last)
+        def _():
+            chain_copy(unit, 1).wait_recv()
+
+        for t in range(channels):
+            own, row, mid, v_south, v_north = merid_terms(
+                spec, unit, t, filt, sides, chain_recv.at[0, unit], chain_recv.at[1, unit], 2 * t,
+            )
+            work[lat_rows * t:lat_rows * (t + 1), :] = mid
+            rim = rim_at + lat_rows * t + 2 * unit
+            work[rim:rim + 1, :] = v_south
+            work[rim + 1:rim + 2, :] = v_north
+        inverse(2 if unit == units - 1 else 1)
+        put_blocks(vs, inverse_blocks(back, rows_ref, 0), unit, units)
+        scatter(vs, vr, 4, unit)
+    rims = inverse_blocks(back, rows_ref, rim_at)
+    for b, value in enumerate(rims):
+        rim_send[b // split, :, (b % split) * LANE:(b % split + 1) * LANE] = value
+
+    last_scatter(rim_send, rim_recv, 1)
+
+    def last_wait(target, sems, n):
+        block = target.at[pl.ds(0, per_band - 1)]
+        pltpu.make_async_copy(block, block, sems.at[n]).wait()
+
     for unit in range(units):
         gathered(ur, 3, unit)
-        gathered(vr, 4, unit)
         for d in range(per_band):
             level = d * units + unit
             u_out[level] = u_ref[level] + ur[level]
+    last_wait(border_recv, last_recv, 0)
+    added_borders(own_ref, border_recv, base, units)
+    for unit in range(units):
+        gathered(vr, 4, unit)
+        own_levels = [d * units + unit for d in range(per_band)]
+        for level in own_levels:
             v_out[level] = v_ref[level] + vr[level]
-    for n, target in enumerate((border_recv, rim_recv)):
-        block = target.at[pl.ds(0, per_band - 1)]
-        pltpu.make_async_copy(block, block, last_recv.at[n]).wait()
-    added_divergence(ur, vr, own_ref, border_recv, rim_recv, base, units)
+        added_divergence(ur, vr, own_ref, base, own_levels)
+    last_wait(rim_recv, last_recv, 1)
+    added_rims(own_ref, rim_recv, base, units)
     solve_columns(a_ref, s_ref, w_mid, p_mid, (base,), ratio, inv, w_out, p_out)
     for source, sem in ((p_ref, 0), (ds1, 1), (p_mid, 2), (us, 3), (vs, 4)):
         sent(source, sem)
-    for n, source in enumerate((border_send, rim_send)):
-        block = source.at[pl.ds(0, per_band - 1)]
-        pltpu.make_async_copy(block, block, last_send.at[n]).wait()
-    for phase in range(2):
-        halo_wait(phase, halo_send, True)
+    last_wait(border_send, last_send, 0)
+    last_wait(rim_send, last_send, 1)
+    halo_wait(halo_send, True)
     for copy in edge_copies:
         copy.wait_send()
 
     @pl.when(not_first)
     def _():
+        pltpu.make_async_copy(chain_send.at[1], chain_send.at[1], chain_out.at[1]).wait()
         coef_copy(-1, 1).wait_send()
         row_copy(-1, 0).wait_send()
 
     @pl.when(not_last)
     def _():
+        pltpu.make_async_copy(chain_send.at[0], chain_send.at[0], chain_out.at[0]).wait()
         coef_copy(1, 0).wait_send()
         row_copy(1, 1).wait_send()
 
@@ -834,7 +902,8 @@
 
     field = scratch(*pressure.shape)
     halo = scratch(2, per_band, lat_rows, width)
-    spare = scratch(whole_tiles(3 * per_unit), TILE)
+    chain = scratch(2, units, -(-2 * channels // 8) * 8, TILE)
+    spare = scratch(whole_tiles(2 * per_unit), TILE)
     dma = pltpu.SemaphoreType.DMA
     operands = (
         level_coef, zonal_coef, merid_coef, cutoff, filter_mask,
@@ -845,19 +914,19 @@
         out_shape=(pltpu.VMEM(pressure.shape, jnp.float32),) * 4,
         in_specs=[far] * len(operands),
         out_specs=(vmem,) * 4,
-        scratch_shapes=[field] * 18 + [halo] * 4 + [
+        scratch_shapes=[field] * 18 + [halo, scratch(per_band, lat_rows, width), scratch(per_band, lat_rows, width), chain, chain] + [
             pltpu.VMEM(table.shape, table.dtype), scratch(*rows.shape),
             scratch(units + 2, per_unit, TILE), spare, spare,
             scratch(channels, 3, lat_rows, TILE), scratch(channels, 8, TILE),
             scratch(3, lat_rows, LANE), scratch(2, 3, lat_rows, LANE),
             scratch(2, lat_rows, LANE), scratch(2, lat_rows, LANE),
             scratch(2, levels, width), scratch(2, levels, width),
-            scratch(per_band, lat_rows, LANE), scratch(per_band, lat_rows, LANE),
+            scratch(per_band, lat_rows, LANE), scratch(per_band, 1, LANE), scratch(per_band, 1, LANE),
             scratch(per_band, lat_rows, width), scratch(per_band, lat_rows, width),
             pltpu.SMEM(level_coef.shape, jnp.float32), pltpu.SMEM(zonal_coef.shape, jnp.float32),
             pltpu.SMEM(merid_coef.shape, jnp.float32), pltpu.SMEM(cutoff.shape, jnp.int32),
             pltpu.SMEM(filter_mask.shape, jnp.int32),
-            dma((len(operands),)), dma((5,)), dma((5, units)), dma((6,)), dma((6,)), dma((4,)), dma((4,)), dma((2,)), dma((2,)),
+            dma((len(operands),)), dma((5,)), dma((5, units)), dma((6,)), dma((6,)), dma((2,)), dma((2,)), dma((2,)), dma((2,)), dma((2,)), dma((2, units)),
         ],
         compiler_params=pltpu.CompilerParams(collective_id=0, has_side_effects=True, vmem_limit_bytes=FUSED_VMEM),
     )(*[pltpu.with_memory_space_constraint(x, pltpu.HBM) for x in operands])

time: 32.1 us -> 30.8 us (0.960)
  Pallas kernels: 31.3 us -> 30 us
    pallas_call x1, Pallas kernels: 30.3 us -> 29 us  [level_body(): pl.pallas_call(functools.partial(fused_kernel, bands, per_band), out_shap...]
where the time goes in v2:
time: 30.8 us; the launch traced here: 30.7 us
  Pallas kernels  30 us (97%)
  between operations  0.64 us (2%)
    pallas_call x1, Pallas kernels, level_body(): pl.pallas_call(functools.partial(fused_kernel, bands, per_band), out_shap...  29 us
    pallas_call x1, Pallas kernels, deliver(): pl.pallas_call(deliver_kernel, out_shape=tuple((jax.ShapeDtypeStruct(a.sh...  1 us

profile of v2, /device:TPU:0, one launch (start us, length us, event | category | flops | bytes accessed | tf_op | source)
XLA Modules:
  0.0 30.7 jit_solution(1753945782164555691)
XLA Ops:
  0.6 29.0 %shard_map.147 = (f32[32,8,256]{2,1,0:T(8,128)S(1)}, f32[32,8,256]{2,1,0:T(8,128)S(1)}, f32[32,8,256]{2,1,0:T(8,128)S(1)}, f32[32,8,256]{2,1,0:T(8,128)S(1)}) custom-call(f32[32]{0:T(128)} %a_far.1, f32[8]{0:T(128)} %zc_far.1, f32[8]{0:T(128)} %mc_far.1, s32[32]{0:T(128)} %cutoff_far.1, s32[32]{0:T(128)} %mask_far.1, f32[32,8,256]{2,1,0:T(8,128)} %u_far.1, ...), custom_call_target="tpu_custom_call" | custom-call | tf_op jit(solution)/shard_map/pallas_call | solution.py:912
  29.7 1.0 %shard_map.148 = (f32[32,8,256]{2,1,0:T(8,128)}, f32[32,8,256]{2,1,0:T(8,128)}, f32[32,8,256]{2,1,0:T(8,128)}, f32[32,8,256]{2,1,0:T(8,128)}) custom-call(f32[32,8,256]{2,1,0:T(8,128)S(1)} %get-tuple-element.8.refs_0_, f32[32,8,256]{2,1,0:T(8,128)S(1)} %get-tuple-element.9.refs_1_, f32[32,8,256]{2,1,0:T(8,128)S(1)} %get-tuple-element.10.refs_2_, ...), custom_call_target="tpu_custom_call" | custom-call | tf_op jit(solution)/shard_map/pallas_call | solution.py:867

commit v3 on v2

--- a/solution.py
+++ b/solution.py
@@ -352,7 +352,7 @@
     return own, row, mid, v_south, v_north
 
 
-def factor_columns(a_ref, s_ref, ratio_ref, inv_ref):
+def factor_columns(a_ref, s_ref, ratio_ref, inv_ref, gain_ref, carry_ref):
     levels = s_ref.shape[0]
     prev = jnp.zeros(s_ref.shape[1:], jnp.float32)
     for level in range(levels):
@@ -363,29 +363,22 @@
         prev = -above * inv
         ratio_ref[level] = prev
         inv_ref[level] = inv
-
-
-def solve_columns(a_ref, s_ref, w_ref, p_ref, parts, ratio_ref, inv_ref, w_out, p_out):
+        gain_ref[level] = alpha * inv
+        carry_ref[level] = below * inv
+
+
+def solve_columns(s_ref, winv_ref, p_ref, spread, ratio_ref, gain_ref, carry_ref, w_out, p_out):
     levels = s_ref.shape[0]
 
     def star(level):
-        total = parts[0][level]
-        for part in parts[1:]:
-            total = total + part[level]
-        return p_ref[level] - s_ref[level] * total
+        return p_ref[level] - s_ref[level] * spread(level)
 
     here = star(0)
     prev = jnp.zeros_like(here)
     for level in range(levels):
-        alpha = a_ref[level]
         p_out[level] = here
-        if level + 1 < levels:
-            nxt = star(level + 1)
-            rhs = w_ref[level] - alpha * (nxt - here)
-        else:
-            nxt = here
-            rhs = w_ref[level] + alpha * here
-        prev = (rhs + alpha * s_ref[level] * prev) * inv_ref[level]
+        nxt = star(level + 1) if level + 1 < levels else jnp.zeros_like(here)
+        prev = (winv_ref[level] - gain_ref[level] * (nxt - here)) + carry_ref[level] * prev
         w_out[level] = prev
         here = nxt
     upper = w_out[levels - 1]
@@ -395,6 +388,22 @@
         p_out[level] = p_out[level] - s_ref[level] * (upper - lower)
         upper = lower
     p_out[0] = p_out[0] - s_ref[0] * upper
+
+
+def paired_rows(first, second, inner):
+    row = lax.broadcasted_iota(jnp.int32, first.shape, 0)
+    rows = first.shape[0]
+    shift = 2 if not inner else rows - 2
+    return jnp.where(row < rows // 2, pltpu.roll(first, shift, 0), pltpu.roll(second, rows - shift, 0))
+
+
+def unpaired_rows(tile, second, inner):
+    rows = tile.shape[0]
+    row = lax.broadcasted_iota(jnp.int32, tile.shape, 0)
+    middle = jnp.logical_and(row >= 2, row < rows - 2)
+    shift = rows - 2 if second == inner else 2
+    moved = pltpu.roll(tile, shift, 0)
+    return jnp.where(middle, moved, 0.0) if inner else jnp.where(middle, 0.0, moved)
 
 
 def divergence(u, v, zonal, merid, west, east, south, north):
@@ -439,16 +448,6 @@
             east = jnp.where(lane == LANE - 1, zonal * border[:, 2 * l + 1:2 * l + 2], 0.0)
             base_ref[level, :, :LANE] = base_ref[level, :, :LANE] - west
             base_ref[level, :, width - LANE:] = base_ref[level, :, width - LANE:] + east
-
-
-def added_rims(own_ref, rim_ref, base_ref, units):
-    merid = own_ref[1, :, 0:1]
-    rows = base_ref.shape[1]
-    for d in range(rim_ref.shape[0]):
-        for l in range(units):
-            level = d * units + l
-            base_ref[level, 0:1, :] = base_ref[level, 0:1, :] - merid[0:1] * rim_ref[d, 2 * l:2 * l + 1, :]
-            base_ref[level, rows - 1:rows, :] = base_ref[level, rows - 1:rows, :] + merid[rows - 1:rows] * rim_ref[d, 2 * l + 1:2 * l + 2, :]
 
 
 def pack_edges(u_ref, v_ref, first_col, last_col, first_row, last_row):
@@ -500,17 +499,17 @@
 
 
 def partner_masks(count):
-    return sorted(range(1, count), key=lambda mask: (-bin(mask // 2).count("1"), mask % 2, mask))
+    return sorted(range(1, count), key=lambda mask: (-bin(mask // 2).count("1"), -(mask % 2), -mask))
 
 
 def fused_kernel(
     bands, per_band, a_far, zc_far, mc_far, cutoff_far, mask_far, u_far, v_far, w_far, p_far, s_far, table_far, rows_far,
-    u_out, v_out, w_out, p_out,
-    x1, x2, d1, ur, vr, ds1, us, vs, w_mid, p_mid, base, ratio, inv, u_ref, v_ref, w_ref, p_ref, s_ref,
+    u_out, v_out, base, winv, p_mid, s_ref, ratio, gain, carry, own_ref, rim_recv,
+    x1, x2, d1, ur, vr, ds1, us, vs, w_mid, inv, u_ref, v_ref, w_ref, p_ref,
     halo1, low, high, chain_send, chain_recv, table_ref, rows_ref, spec, work, back, filt, sides,
-    own_ref, near, cols_send, cols_recv, rows_send, rows_recv, border_tile, border_send, border_recv, rim_send, rim_recv,
+    near, cols_send, cols_recv, rows_send, rows_recv, border_tile, border_send, border_recv, rim_send,
     a_ref, zc_ref, mc_ref, cutoff_ref, mask_ref,
-    load_sems, send_sems, recv_sems, edge_send, edge_recv, halo_send, halo_recv, last_send, last_recv, chain_out, chain_in,
+    load_sems, send_sems, recv_sems, edge_send, edge_recv, halo_send, halo_recv, last_send, last_recv, chain_out, chain_in, band_in,
 ):
     band_me = lax.axis_index("lat")
     lon_me = lax.axis_index("lon")
@@ -545,25 +544,29 @@
     for there, step in ((not_first, -1), (not_last, 1)):
         @pl.when(there)
         def _():
-            for other in partners + [lon_me]:
-                greet(band_me + step, other)
+            greet(band_me + step, lon_me)
 
     loads[0].wait()
     pack_halo(p_ref, low, high, units)
-    expected = per_band - 1 + jnp.where(is_first, 0, per_band) + jnp.where(is_last, 0, per_band)
-    pl.semaphore_wait(barrier, expected)
-
-    def scatter(source, target, sem, unit):
+    pl.semaphore_wait(barrier, per_band - 1 + jnp.where(is_first, 0, 1) + jnp.where(is_last, 0, 1))
+    for there, step, place in ((not_first, -1, 1), (not_last, 1, 0)):
+        @pl.when(there)
+        def _():
+            pl.semaphore_signal(band_in.at[place], inc=1, device_id=(band_me + step, lon_me), device_id_type=mesh_id)
+
+
+    def scatter(source, target, sem, unit, count=1):
         for g in partners:
             pltpu.make_async_remote_copy(
-                src_ref=source.at[pl.ds(g * units + unit, 1)], dst_ref=target.at[pl.ds(lon_me * units + unit, 1)],
+                src_ref=source.at[pl.ds(g * units + unit, count)], dst_ref=target.at[pl.ds(lon_me * units + unit, count)],
                 send_sem=send_sems.at[sem], recv_sem=recv_sems.at[sem, unit],
                 device_id=(band_me, g), device_id_type=mesh_id,
             ).start()
-        target[lon_me * units + unit] = source[lon_me * units + unit]
-
-    def gathered(target, sem, unit):
-        block = target.at[pl.ds(0, per_band - 1)]
+        for n in range(count):
+            target[lon_me * units + unit + n] = source[lon_me * units + unit + n]
+
+    def gathered(target, sem, unit, count=1):
+        block = target.at[pl.ds(0, (per_band - 1) * count)]
         pltpu.make_async_copy(block, block, recv_sems.at[sem, unit]).wait()
 
     def sent(source, sem):
@@ -581,10 +584,12 @@
 
         @pl.when(not_first)
         def _():
+            pl.semaphore_wait(band_in.at[0], 1)
             one(low, 1, 0, band_me - 1)
 
         @pl.when(not_last)
         def _():
+            pl.semaphore_wait(band_in.at[1], 1)
             one(high, 0, 1, band_me + 1)
 
     def halo_wait(sems, upward):
@@ -609,9 +614,9 @@
             device_id=((band_me + bands + step) % bands, lon_me), device_id_type=mesh_id,
         )
 
-    spread_halo(halo1)
     for unit in range(units):
         scatter(p_ref, x1, 0, unit)
+    spread_halo(halo1)
 
     for load in loads[1:7]:
         load.wait()
@@ -676,7 +681,9 @@
 
     for load in loads[9:]:
         load.wait()
-    factor_columns(a_ref, s_ref, ratio, inv)
+    factor_columns(a_ref, s_ref, ratio, inv, gain, carry)
+    for level in range(s_ref.shape[0]):
+        winv[level] = w_ref[level] * inv[level]
 
     @pl.when(not_first)
     def _():
@@ -741,9 +748,15 @@
     )
     for unit in range(units):
         gathered(d1, 1, unit)
-    solve_columns(a_ref, s_ref, w_ref, p_ref, (base, d1), ratio, inv, w_mid, p_mid)
+
+    def first_spread(level):
+        return base[level] + d1[level]
+
+    solve_columns(s_ref, winv, p_ref, first_spread, ratio, gain, carry, vs, p_mid)
     for unit in range(units):
         scatter(p_mid, x2, 2, unit)
+    for level in range(s_ref.shape[0]):
+        winv[level] = vs[level] * inv[level]
 
     zonal = own_ref[0, :, 0:1]
     for unit in range(units):
@@ -829,8 +842,6 @@
             v_out[level] = v_ref[level] + vr[level]
         added_divergence(ur, vr, own_ref, base, own_levels)
     last_wait(rim_recv, last_recv, 1)
-    added_rims(own_ref, rim_recv, base, units)
-    solve_columns(a_ref, s_ref, w_mid, p_mid, (base,), ratio, inv, w_out, p_out)
     for source, sem in ((p_ref, 0), (ds1, 1), (p_mid, 2), (us, 3), (vs, 4)):
         sent(source, sem)
     last_wait(border_send, last_send, 0)
@@ -852,24 +863,40 @@
         row_copy(1, 1).wait_send()
 
 
-def deliver_kernel(*refs):
-    count = (len(refs) - 1) // 2
-    sems = refs[-1]
-    copies = [pltpu.make_async_copy(refs[n], refs[count + n], sems.at[n]) for n in range(count)]
-    for copy in copies:
-        copy.start()
+def deliver_kernel(
+    units, u_ref, v_ref, base, winv, p_mid, s_ref, ratio, gain, carry, own_ref, rim_ref, u_out, v_out, w_out, p_out, w_end, p_end, sems,
+):
+    copies = [
+        pltpu.make_async_copy(source, target, sems.at[n])
+        for n, (source, target) in enumerate(((u_ref, u_out), (v_ref, v_out), (w_end, w_out), (p_end, p_out)))
+    ]
+    copies[0].start()
+    copies[1].start()
+    row = lax.broadcasted_iota(jnp.int32, u_ref.shape[1:], 0)
+    rows = u_ref.shape[1]
+    merid = own_ref[1, :, 0:1]
+    south = jnp.where(row == 0, -merid, 0.0)
+    north = jnp.where(row == rows - 1, merid, 0.0)
+
+    def spread(level):
+        d, l = level // units, 2 * (level % units)
+        return base[level] + south * rim_ref[d, l:l + 1, :] + north * rim_ref[d, l + 1:l + 2, :]
+
+    solve_columns(s_ref, winv, p_mid, spread, ratio, gain, carry, w_end, p_end)
+    copies[2].start()
+    copies[3].start()
     for copy in copies:
         copy.wait()
 
 
-def deliver(arrays):
-    count = len(arrays)
+def deliver(units, arrays):
+    shape = arrays[0].shape
     return pl.pallas_call(
-        deliver_kernel,
-        out_shape=tuple(jax.ShapeDtypeStruct(a.shape, a.dtype) for a in arrays),
-        in_specs=[pl.BlockSpec(memory_space=pltpu.VMEM)] * count,
-        out_specs=(pl.BlockSpec(memory_space=pl.ANY),) * count,
-        scratch_shapes=[pltpu.SemaphoreType.DMA((count,))],
+        functools.partial(deliver_kernel, units),
+        out_shape=(jax.ShapeDtypeStruct(shape, jnp.float32),) * 4,
+        in_specs=[pl.BlockSpec(memory_space=pltpu.VMEM)] * len(arrays),
+        out_specs=(pl.BlockSpec(memory_space=pl.ANY),) * 4,
+        scratch_shapes=[pltpu.VMEM(shape, jnp.float32)] * 2 + [pltpu.SemaphoreType.DMA((4,))],
         compiler_params=pltpu.CompilerParams(vmem_limit_bytes=FINISH_VMEM),
     )(*arrays)
 
@@ -911,26 +938,29 @@
     )
     results = pl.pallas_call(
         functools.partial(fused_kernel, bands, per_band),
-        out_shape=(pltpu.VMEM(pressure.shape, jnp.float32),) * 4,
+        out_shape=(pltpu.VMEM(pressure.shape, jnp.float32),) * 9 + (
+            pltpu.VMEM((3, lat_rows, LANE), jnp.float32), pltpu.VMEM((per_band, lat_rows, width), jnp.float32),
+        ),
         in_specs=[far] * len(operands),
-        out_specs=(vmem,) * 4,
-        scratch_shapes=[field] * 18 + [halo, scratch(per_band, lat_rows, width), scratch(per_band, lat_rows, width), chain, chain] + [
+        out_specs=(vmem,) * 11,
+        scratch_shapes=[field] * 14 + [halo, scratch(per_band, lat_rows, width), scratch(per_band, lat_rows, width), chain, chain] + [
             pltpu.VMEM(table.shape, table.dtype), scratch(*rows.shape),
             scratch(units + 2, per_unit, TILE), spare, spare,
             scratch(channels, 3, lat_rows, TILE), scratch(channels, 8, TILE),
-            scratch(3, lat_rows, LANE), scratch(2, 3, lat_rows, LANE),
+            scratch(2, 3, lat_rows, LANE),
             scratch(2, lat_rows, LANE), scratch(2, lat_rows, LANE),
             scratch(2, levels, width), scratch(2, levels, width),
             scratch(per_band, lat_rows, LANE), scratch(per_band, 1, LANE), scratch(per_band, 1, LANE),
-            scratch(per_band, lat_rows, width), scratch(per_band, lat_rows, width),
+            scratch(per_band, lat_rows, width),
             pltpu.SMEM(level_coef.shape, jnp.float32), pltpu.SMEM(zonal_coef.shape, jnp.float32),
             pltpu.SMEM(merid_coef.shape, jnp.float32), pltpu.SMEM(cutoff.shape, jnp.int32),
             pltpu.SMEM(filter_mask.shape, jnp.int32),
             dma((len(operands),)), dma((5,)), dma((5, units)), dma((6,)), dma((6,)), dma((2,)), dma((2,)), dma((2,)), dma((2,)), dma((2,)), dma((2, units)),
+            pltpu.SemaphoreType.REGULAR((2,)),
         ],
         compiler_params=pltpu.CompilerParams(collective_id=0, has_side_effects=True, vmem_limit_bytes=FUSED_VMEM),
     )(*[pltpu.with_memory_space_constraint(x, pltpu.HBM) for x in operands])
-    return deliver(results)
+    return deliver(units, results)
 
 
 def body(tables, *arrays):

time: 30.8 us -> 29.9 us (0.971)
  Pallas kernels: 30 us -> 29.1 us
    pallas_call x1, Pallas kernels: 29 us -> 28 us  [level_body(): pl.pallas_call(functools.partial(fused_kernel, bands, per_band), out_shap...]
where the time goes in v3:
time: 29.9 us; the launch traced here: 29.8 us
  Pallas kernels  29.1 us (97%)
  between operations  0.64 us (2%)
    pallas_call x1, Pallas kernels, level_body(): pl.pallas_call(functools.partial(fused_kernel, bands, per_band), out_shap...  28 us
    pallas_call x1, Pallas kernels, deliver(): pl.pallas_call(functools.partial(deliver_kernel, units), out_shape=(jax.S...  1.09 us

profile of v3, /device:TPU:0, one launch (start us, length us, event | category | flops | bytes accessed | tf_op | source)
XLA Modules:
  0.0 29.8 jit_solution(7209162675698134278)
XLA Ops:
  0.6 28.0 %shard_map.147 = (f32[32,8,256]{2,1,0:T(8,128)S(1)}, f32[32,8,256]{2,1,0:T(8,128)S(1)}, f32[32,8,256]{2,1,0:T(8,128)S(1)}, f32[32,8,256]{2,1,0:T(8,128)S(1)}, f3...) custom-call(f32[32]{0:T(128)} %a_far.1, f32[8]{0:T(128)} %zc_far.1, ...), custom_call_target="tpu_custom_call" | custom-call | tf_op jit(solution)/shard_map/pallas_call | solution.py:939
  28.7 1.1 %shard_map.148 = (f32[32,8,256]{2,1,0:T(8,128)}, f32[32,8,256]{2,1,0:T(8,128)}, f32[32,8,256]{2,1,0:T(8,128)}, f32[32,8,256]{2,1,0:T(8,128)}) custom-call(f32[32,8,256]{2,1,0:T(8,128)S(1)} %get-tuple-element.15.u_ref, f32[32,8,256]{2,1,0:T(8,128)S(1)} %get-tuple-element.16.v_ref, f32[32,8,256]{2,1,0:T(8,128)S(1)} %get-tuple-element.17.base, ...), custom_call_target="tpu_custom_call" | custom-call | tf_op jit(solution)/shard_map/pallas_call | solution.py:894

commit v4 on v3

--- a/solution.py
+++ b/solution.py
@@ -332,6 +332,8 @@
         filt_ref[t, 0] = factor
         filt_ref[t, 1] = merid * factor
         filt_ref[t, 2] = (zonal * zonal) * sines * factor
+        filt_ref[t, 3] = packed_half(factor, factor, False)
+        filt_ref[t, 4] = packed_half(factor, factor, True)
         south = near_ref[0, 1, rows - 1:rows, 0:1] * filter_values(near_ref[0, 2, rows - 1:rows, 0:1], wave, scale)
         north = near_ref[1, 1, 0:1, 0:1] * filter_values(near_ref[1, 2, 0:1, 0:1], wave, scale)
         side_ref[t, 0:1, :] = south
@@ -390,20 +392,19 @@
     p_out[0] = p_out[0] - s_ref[0] * upper
 
 
-def paired_rows(first, second, inner):
+def packed_half(first, second, inner):
+    rows = first.shape[0]
     row = lax.broadcasted_iota(jnp.int32, first.shape, 0)
-    rows = first.shape[0]
-    shift = 2 if not inner else rows - 2
+    shift = rows - 2 if inner else 2
     return jnp.where(row < rows // 2, pltpu.roll(first, shift, 0), pltpu.roll(second, rows - shift, 0))
 
 
-def unpaired_rows(tile, second, inner):
-    rows = tile.shape[0]
-    row = lax.broadcasted_iota(jnp.int32, tile.shape, 0)
+def unpacked(outer, inner, second):
+    rows = outer.shape[0]
+    row = lax.broadcasted_iota(jnp.int32, outer.shape, 0)
+    shift = rows - 2 if second else 2
     middle = jnp.logical_and(row >= 2, row < rows - 2)
-    shift = rows - 2 if second == inner else 2
-    moved = pltpu.roll(tile, shift, 0)
-    return jnp.where(middle, moved, 0.0) if inner else jnp.where(middle, 0.0, moved)
+    return jnp.where(middle, pltpu.roll(inner, shift, 0), pltpu.roll(outer, rows - shift, 0))
 
 
 def divergence(u, v, zonal, merid, west, east, south, north):
@@ -442,10 +443,13 @@
     lane = lax.broadcasted_iota(jnp.int32, (8, LANE), 1)
     for d in range(border_ref.shape[0]):
         border = border_columns(border_ref[d])
+        higher = pltpu.roll(border, LANE - units, 1)
+        sides = [unpacked(border, higher, l == 1) for l in range(2)]
         for l in range(units):
             level = d * units + l
-            west = jnp.where(lane == 0, zonal * border[:, 2 * l:2 * l + 1], 0.0)
-            east = jnp.where(lane == LANE - 1, zonal * border[:, 2 * l + 1:2 * l + 2], 0.0)
+            at = l // 2 * 2
+            west = jnp.where(lane == 0, zonal * sides[l % 2][:, at:at + 1], 0.0)
+            east = jnp.where(lane == LANE - 1, zonal * sides[l % 2][:, at + 1:at + 2], 0.0)
             base_ref[level, :, :LANE] = base_ref[level, :, :LANE] - west
             base_ref[level, :, width - LANE:] = base_ref[level, :, width - LANE:] + east
 
@@ -505,8 +509,8 @@
 def fused_kernel(
     bands, per_band, a_far, zc_far, mc_far, cutoff_far, mask_far, u_far, v_far, w_far, p_far, s_far, table_far, rows_far,
     u_out, v_out, base, winv, p_mid, s_ref, ratio, gain, carry, own_ref, rim_recv,
-    x1, x2, d1, ur, vr, ds1, us, vs, w_mid, inv, u_ref, v_ref, w_ref, p_ref,
-    halo1, low, high, chain_send, chain_recv, table_ref, rows_ref, spec, work, back, filt, sides,
+    x1, x2, d1, ur, vr, ds1, us, vs, w_mid, packed_p, inv, u_ref, v_ref, w_ref, p_ref,
+    halo1, low, high, chain_send, chain_recv, table_ref, rows_ref, spec, packed_spec, work, back, filt, sides,
     near, cols_send, cols_recv, rows_send, rows_recv, border_tile, border_send, border_recv, rim_send,
     a_ref, zc_ref, mc_ref, cutoff_ref, mask_ref,
     load_sems, send_sems, recv_sems, edge_send, edge_recv, halo_send, halo_recv, last_send, last_recv, chain_out, chain_in, band_in,
@@ -532,8 +536,7 @@
         (rows_far, rows_ref), (u_far, u_ref), (v_far, v_ref), (table_far, table_ref), (s_far, s_ref), (w_far, w_ref),
     )
     loads = [pltpu.make_async_copy(far, here, load_sems.at[n]) for n, (far, here) in enumerate(pairs)]
-    for load in loads:
-        load.start()
+    loads[0].start()
     barrier = pltpu.get_barrier_semaphore()
 
     def greet(band, lon):
@@ -546,8 +549,9 @@
         def _():
             greet(band_me + step, lon_me)
 
+    for load in loads[1:]:
+        load.start()
     loads[0].wait()
-    pack_halo(p_ref, low, high, units)
     pl.semaphore_wait(barrier, per_band - 1 + jnp.where(is_first, 0, 1) + jnp.where(is_last, 0, 1))
     for there, step, place in ((not_first, -1, 1), (not_last, 1, 0)):
         @pl.when(there)
@@ -608,14 +612,29 @@
             device_id=((band_me + bands + 1 - 2 * side) % bands, lon_me), device_id_type=mesh_id,
         )
 
+    def chain_start(unit, tile, place):
+        for t in range(channels):
+            at = lat_rows * t + place
+            chain_send[0, unit, 2 * t:2 * t + 2, :] = packed_spec[tile, at:at + 2, :]
+            chain_send[1, unit, 2 * t:2 * t + 2, :] = packed_spec[tile, at + 2:at + 4, :]
+
+        @pl.when(not_last)
+        def _():
+            chain_copy(unit, 0).start()
+
+        @pl.when(not_first)
+        def _():
+            chain_copy(unit, 1).start()
+
     def coef_copy(step, side):
         return pltpu.make_async_remote_copy(
             src_ref=own_ref, dst_ref=near.at[side], send_sem=edge_send.at[4 + side], recv_sem=edge_recv.at[4 + side],
             device_id=((band_me + bands + step) % bands, lon_me), device_id_type=mesh_id,
         )
 
-    for unit in range(units):
-        scatter(p_ref, x1, 0, unit)
+    for unit in range(0, units, 2):
+        scatter(p_ref, x1, 0, unit, 2)
+    pack_halo(p_ref, low, high, units)
     spread_halo(halo1)
 
     for load in loads[1:7]:
@@ -701,35 +720,43 @@
             for n in range(count)
         ]
 
-    def forward(tiles, places, accumulate):
+    def forward(tiles, places):
         for n, xs in enumerate(tiles):
             forward_fill(xs, rows_ref, work, n * per_unit)
         used = len(tiles) * per_unit
         value = three_products(work[0:whole_tiles(used), :], table_ref)
         for n, place in enumerate(places):
-            part = value[n * per_unit:(n + 1) * per_unit]
-            spec[place] = spec[place] + part if accumulate else part
+            spec[place] = value[n * per_unit:(n + 1) * per_unit]
+        return value
 
     def inverse(count):
         back[0:whole_tiles(count * per_unit), :] = three_products(work[0:whole_tiles(count * per_unit), :], table_ref)
 
+    merid = own_ref[1, :, 0:1]
+    pair_count = units // 2
     halo_wait(halo_recv, False)
     forward([
         [halo1[slot, d, :, h * LANE:(h + 1) * LANE] for d in range(per_band) for h in range(split)] for slot in range(2)
-    ], [units, units + 1], False)
-    for unit in range(units):
-        gathered(x1, 0, unit)
-        forward(circles(x1, unit, 1, units), [unit], False)
+    ], [units, units + 1])
+    for pair in range(pair_count):
+        gathered(x1, 0, 2 * pair, 2)
+        forward(circles(x1, 2 * pair, 2, units), [2 * pair, 2 * pair + 1])
         for t in range(channels):
-            at = lat_rows * t + 2 * unit
-            own, row, mid, v_south, v_north = merid_terms(spec, unit, t, filt, sides, spec.at[units], spec.at[units + 1], at)
-            upper = jnp.where(row == lat_rows - 1, v_north, pltpu.roll(mid, lat_rows - 1, 0))
-            lower = jnp.where(row == 0, v_south, pltpu.roll(mid, 1, 0))
-            merid = own_ref[1, :, 0:1]
-            work[lat_rows * t:lat_rows * (t + 1), :] = filt[t, 2] * own + merid * (upper - lower)
-        inverse(1)
-        put_blocks(ds1, inverse_blocks(back, rows_ref, 0), unit, units)
-        scatter(ds1, d1, 1, unit)
+            both = []
+            for l in (2 * pair, 2 * pair + 1):
+                at = lat_rows * t + 2 * l
+                own, row, mid, v_south, v_north = merid_terms(spec, l, t, filt, sides, spec.at[units], spec.at[units + 1], at)
+                upper = jnp.where(row == lat_rows - 1, v_north, pltpu.roll(mid, lat_rows - 1, 0))
+                lower = jnp.where(row == 0, v_south, pltpu.roll(mid, 1, 0))
+                both.append(filt[t, 2] * own + merid * (upper - lower))
+            for half_at in range(2):
+                at = half_at * per_unit + lat_rows * t
+                work[at:at + lat_rows, :] = packed_half(*both, half_at == 1)
+        inverse(2)
+        put_blocks(ds1, inverse_blocks(back, rows_ref, 0), pair, units)
+        scatter(ds1, d1, 1, pair)
+        put_blocks(ds1, inverse_blocks(back, rows_ref, per_unit), pair_count + pair, units)
+        scatter(ds1, d1, 1, pair_count + pair)
 
     for copy in edge_copies:
         copy.wait_recv()
@@ -746,43 +773,48 @@
         u_ref, v_ref, own_ref, cols_recv.at[1], cols_recv.at[0], rows_recv.at[1], rows_recv.at[0], base,
         is_first, is_last,
     )
-    for unit in range(units):
-        gathered(d1, 1, unit)
-
     def first_spread(level):
-        return base[level] + d1[level]
-
-    solve_columns(s_ref, winv, p_ref, first_spread, ratio, gain, carry, vs, p_mid)
-    for unit in range(units):
-        scatter(p_mid, x2, 2, unit)
+        tile = d1[level // units * units + level % units // 2]
+        return base[level] + (pltpu.roll(tile, 2 if level % 2 else lat_rows - 2, 0))
+
+    def second_spread(level):
+        place = level // units * units + level % units // 2
+        return base[level] + unpacked(d1[place], d1[place + pair_count], level % 2 == 1)
+
+    for half_at, spread in enumerate((first_spread, second_spread)):
+        for pair in range(pair_count):
+            gathered(d1, 1, half_at * pair_count + pair)
+        solve_columns(s_ref, winv, p_ref, spread, ratio, gain, carry, vs, p_mid)
+        for pair in range(pair_count):
+            for d in range(per_band):
+                level = d * units + 2 * pair
+                packed_p[d * units + half_at * pair_count + pair] = packed_half(p_mid[level], p_mid[level + 1], half_at == 1)
+            scatter(packed_p, x2, 2, half_at * pair_count + pair)
     for level in range(s_ref.shape[0]):
         winv[level] = vs[level] * inv[level]
 
-    zonal = own_ref[0, :, 0:1]
-    for unit in range(units):
-        gathered(x2, 2, unit)
-        forward(circles(x2, unit, 1, units), [unit], True)
+    for tile in range(units):
+        pair, half_at = tile % pair_count, tile // pair_count
+        gathered(x2, 2, tile)
+        value = forward(circles(x2, tile, 1, units), [])
         for t in range(channels):
-            at = lat_rows * t
-            chain_send[0, unit, 2 * t:2 * t + 2, :] = spec[unit, at + lat_rows - 2:at + lat_rows, :]
-            chain_send[1, unit, 2 * t:2 * t + 2, :] = spec[unit, at:at + 2, :]
-
-        @pl.when(not_last)
-        def _():
-            chain_copy(unit, 0).start()
-
-        @pl.when(not_first)
-        def _():
-            chain_copy(unit, 1).start()
-
-        for t in range(channels):
-            at = lat_rows * t
-            work[at:at + lat_rows, :] = filt[t, 0] * spec[unit, at:at + lat_rows, :]
+            rows = slice(lat_rows * t, lat_rows * (t + 1))
+            total = packed_half(spec[2 * pair, rows, :], spec[2 * pair + 1, rows, :], half_at == 1) + value[rows]
+            packed_spec[tile, rows, :] = total
+            work[rows, :] = filt[t, 3 + half_at] * total
+        for l in range(2):
+            if not half_at:
+                chain_start(2 * pair + l, tile, 4 * l)
+                continue
+            for t in range(channels):
+                rows = slice(lat_rows * t, lat_rows * (t + 1))
+                spec[2 * pair + l, rows, :] = unpacked(packed_spec[pair, rows, :], packed_spec[tile, rows, :], l == 1)
+        zonal = packed_half(own_ref[0], own_ref[0], half_at == 1)
         inverse(1)
         moved = [-zonal * x for x in circle_diff(inverse_blocks(back, rows_ref, 0))]
-        put_blocks(us, moved, unit, units)
-        scatter(us, ur, 3, unit)
-        border_tiles(border_tile, moved, unit)
+        put_blocks(us, moved, tile, units)
+        scatter(us, ur, 3, tile)
+        border_tiles(border_tile, moved, tile)
     border_rows(border_tile, border_send)
 
     def last_copy(source, target, n, g):
@@ -828,11 +860,14 @@
         block = target.at[pl.ds(0, per_band - 1)]
         pltpu.make_async_copy(block, block, sems.at[n]).wait()
 
-    for unit in range(units):
-        gathered(ur, 3, unit)
-        for d in range(per_band):
-            level = d * units + unit
-            u_out[level] = u_ref[level] + ur[level]
+    for tile in range(units):
+        gathered(ur, 3, tile)
+        for d in range(per_band if tile >= pair_count else 0):
+            for l in range(2):
+                level = d * units + 2 * (tile - pair_count) + l
+                moved = unpacked(ur[d * units + tile - pair_count], ur[d * units + tile], l == 1)
+                u_out[level] = u_ref[level] + moved
+                w_mid[level] = moved
     last_wait(border_recv, last_recv, 0)
     added_borders(own_ref, border_recv, base, units)
     for unit in range(units):
@@ -840,9 +875,9 @@
         own_levels = [d * units + unit for d in range(per_band)]
         for level in own_levels:
             v_out[level] = v_ref[level] + vr[level]
-        added_divergence(ur, vr, own_ref, base, own_levels)
+        added_divergence(w_mid, vr, own_ref, base, own_levels)
     last_wait(rim_recv, last_recv, 1)
-    for source, sem in ((p_ref, 0), (ds1, 1), (p_mid, 2), (us, 3), (vs, 4)):
+    for source, sem in ((p_ref, 0), (ds1, 1), (packed_p, 2), (us, 3), (vs, 4)):
         sent(source, sem)
     last_wait(border_send, last_send, 0)
     last_wait(rim_send, last_send, 1)
@@ -943,10 +978,10 @@
         ),
         in_specs=[far] * len(operands),
         out_specs=(vmem,) * 11,
-        scratch_shapes=[field] * 14 + [halo, scratch(per_band, lat_rows, width), scratch(per_band, lat_rows, width), chain, chain] + [
+        scratch_shapes=[field] * 15 + [halo, scratch(per_band, lat_rows, width), scratch(per_band, lat_rows, width), chain, chain] + [
             pltpu.VMEM(table.shape, table.dtype), scratch(*rows.shape),
-            scratch(units + 2, per_unit, TILE), spare, spare,
-            scratch(channels, 3, lat_rows, TILE), scratch(channels, 8, TILE),
+            scratch(units + 2, per_unit, TILE), scratch(units, per_unit, TILE), spare, spare,
+            scratch(channels, 5, lat_rows, TILE), scratch(channels, 8, TILE),
             scratch(2, 3, lat_rows, LANE),
             scratch(2, lat_rows, LANE), scratch(2, lat_rows, LANE),
             scratch(2, levels, width), scratch(2, levels, width),
@@ -967,7 +1002,7 @@
     pressure = arrays[3]
     per_band = lax.axis_size("lon")
     levels, lat_rows, width = pressure.shape
-    fits = lat_rows == 8 and levels == 4 * per_band and levels <= LANE and width % LANE == 0 and per_band & (per_band - 1) == 0
+    fits = lat_rows == 8 and levels == 4 * per_band and levels <= LANE and width % LANE == 0 and per_band == 8
     if fits:
         return level_body(tables, *arrays)
     return wide_body(*arrays)

time: 29.9 us -> 29.6 us (0.990)
  Pallas kernels: 29.1 us -> 28.8 us
    pallas_call x1, Pallas kernels: 28 us -> 27.7 us  [level_body(): pl.pallas_call(functools.partial(fused_kernel, bands, per_band), out_shap...]
where the time goes in v4:
time: 29.6 us; the launch traced here: 29.4 us
  Pallas kernels  28.8 us (97%)
  between operations  0.64 us (2%)
    pallas_call x1, Pallas kernels, level_body(): pl.pallas_call(functools.partial(fused_kernel, bands, per_band), out_shap...  27.7 us
    pallas_call x1, Pallas kernels, deliver(): pl.pallas_call(functools.partial(deliver_kernel, units), out_shape=(jax.S...  1.09 us

profile of v4, /device:TPU:0, one launch (start us, length us, event | category | flops | bytes accessed | tf_op | source)
XLA Modules:
  0.0 29.4 jit_solution(174857002496654276)
XLA Ops:
  0.6 27.7 %shard_map.147 = (f32[32,8,256]{2,1,0:T(8,128)S(1)}, f32[32,8,256]{2,1,0:T(8,128)S(1)}, f32[32,8,256]{2,1,0:T(8,128)S(1)}, f32[32,8,256]{2,1,0:T(8,128)S(1)}, f3...) custom-call(f32[32]{0:T(128)} %a_far.1, f32[8]{0:T(128)} %zc_far.1, ...), custom_call_target="tpu_custom_call" | custom-call | tf_op jit(solution)/shard_map/pallas_call | solution.py:974
  28.3 1.1 %shard_map.148 = (f32[32,8,256]{2,1,0:T(8,128)}, f32[32,8,256]{2,1,0:T(8,128)}, f32[32,8,256]{2,1,0:T(8,128)}, f32[32,8,256]{2,1,0:T(8,128)}) custom-call(f32[32,8,256]{2,1,0:T(8,128)S(1)} %get-tuple-element.15.u_ref, f32[32,8,256]{2,1,0:T(8,128)S(1)} %get-tuple-element.16.v_ref, f32[32,8,256]{2,1,0:T(8,128)S(1)} %get-tuple-element.17.base, ...), custom_call_target="tpu_custom_call" | custom-call | tf_op jit(solution)/shard_map/pallas_call | solution.py:929

commit v5 on v4

--- a/solution.py
+++ b/solution.py
@@ -503,7 +503,7 @@
 
 
 def partner_masks(count):
-    return sorted(range(1, count), key=lambda mask: (-bin(mask // 2).count("1"), -(mask % 2), -mask))
+    return sorted(range(1, count), key=lambda mask: (-bin(mask // 2).count("1"), mask % 2, mask))
 
 
 def fused_kernel(
@@ -756,6 +756,7 @@
         put_blocks(ds1, inverse_blocks(back, rows_ref, 0), pair, units)
         scatter(ds1, d1, 1, pair)
         put_blocks(ds1, inverse_blocks(back, rows_ref, per_unit), pair_count + pair, units)
+    for pair in range(pair_count):
         scatter(ds1, d1, 1, pair_count + pair)
 
     for copy in edge_copies:

time: 29.6 us -> 29.1 us (0.983)
  Pallas kernels: 28.8 us -> 28.3 us
    pallas_call x1, Pallas kernels: 27.7 us -> 27.2 us  [level_body(): pl.pallas_call(functools.partial(fused_kernel, bands, per_band), out_shap...]
where the time goes in v5:
time: 29.1 us; the launch traced here: 28.9 us
  Pallas kernels  28.3 us (97%)
  between operations  0.64 us (2%)
    pallas_call x1, Pallas kernels, level_body(): pl.pallas_call(functools.partial(fused_kernel, bands, per_band), out_shap...  27.2 us
    pallas_call x1, Pallas kernels, deliver(): pl.pallas_call(functools.partial(deliver_kernel, units), out_shape=(jax.S...  1.09 us

profile of v5, /device:TPU:0, one launch (start us, length us, event | category | flops | bytes accessed | tf_op | source)
XLA Modules:
  0.0 28.9 jit_solution(1110020443795062868)
XLA Ops:
  0.6 27.2 %shard_map.147 = (f32[32,8,256]{2,1,0:T(8,128)S(1)}, f32[32,8,256]{2,1,0:T(8,128)S(1)}, f32[32,8,256]{2,1,0:T(8,128)S(1)}, f32[32,8,256]{2,1,0:T(8,128)S(1)}, f3...) custom-call(f32[32]{0:T(128)} %a_far.1, f32[8]{0:T(128)} %zc_far.1, ...), custom_call_target="tpu_custom_call" | custom-call | tf_op jit(solution)/shard_map/pallas_call | solution.py:975
  27.8 1.1 %shard_map.148 = (f32[32,8,256]{2,1,0:T(8,128)}, f32[32,8,256]{2,1,0:T(8,128)}, f32[32,8,256]{2,1,0:T(8,128)}, f32[32,8,256]{2,1,0:T(8,128)}) custom-call(f32[32,8,256]{2,1,0:T(8,128)S(1)} %get-tuple-element.15.u_ref, f32[32,8,256]{2,1,0:T(8,128)S(1)} %get-tuple-element.16.v_ref, f32[32,8,256]{2,1,0:T(8,128)S(1)} %get-tuple-element.17.base, ...), custom_call_target="tpu_custom_call" | custom-call | tf_op jit(solution)/shard_map/pallas_call | solution.py:930

commit v6 on v5

--- a/solution.py
+++ b/solution.py
@@ -790,13 +790,19 @@
             for d in range(per_band):
                 level = d * units + 2 * pair
                 packed_p[d * units + half_at * pair_count + pair] = packed_half(p_mid[level], p_mid[level + 1], half_at == 1)
-            scatter(packed_p, x2, 2, half_at * pair_count + pair)
+            if not half_at:
+                scatter(packed_p, x2, 2, pair)
+        if half_at:
+            scatter(packed_p, x2, 2, pair_count, pair_count)
     for level in range(s_ref.shape[0]):
         winv[level] = vs[level] * inv[level]
 
     for tile in range(units):
         pair, half_at = tile % pair_count, tile // pair_count
-        gathered(x2, 2, tile)
+        if not half_at:
+            gathered(x2, 2, tile)
+        elif pair == 0:
+            gathered(x2, 2, tile, pair_count)
         value = forward(circles(x2, tile, 1, units), [])
         for t in range(channels):
             rows = slice(lat_rows * t, lat_rows * (t + 1))

time: 29.1 us -> 29.1 us (level)
  no operation moved by 1% of the time
where the time goes in v6:
time: 29.1 us; the launch traced here: 28.9 us
  Pallas kernels  28.3 us (97%)
  between operations  0.64 us (2%)
    pallas_call x1, Pallas kernels, level_body(): pl.pallas_call(functools.partial(fused_kernel, bands, per_band), out_shap...  27.2 us
    pallas_call x1, Pallas kernels, deliver(): pl.pallas_call(functools.partial(deliver_kernel, units), out_shape=(jax.S...  1.09 us

profile of v6, /device:TPU:0, one launch (start us, length us, event | category | flops | bytes accessed | tf_op | source)
XLA Modules:
  0.0 28.9 jit_solution(9854275933218782714)
XLA Ops:
  0.6 27.2 %shard_map.147 = (f32[32,8,256]{2,1,0:T(8,128)S(1)}, f32[32,8,256]{2,1,0:T(8,128)S(1)}, f32[32,8,256]{2,1,0:T(8,128)S(1)}, f32[32,8,256]{2,1,0:T(8,128)S(1)}, f3...) custom-call(f32[32]{0:T(128)} %a_far.1, f32[8]{0:T(128)} %zc_far.1, ...), custom_call_target="tpu_custom_call" | custom-call | tf_op jit(solution)/shard_map/pallas_call | solution.py:981
  27.8 1.1 %shard_map.148 = (f32[32,8,256]{2,1,0:T(8,128)}, f32[32,8,256]{2,1,0:T(8,128)}, f32[32,8,256]{2,1,0:T(8,128)}, f32[32,8,256]{2,1,0:T(8,128)}) custom-call(f32[32,8,256]{2,1,0:T(8,128)S(1)} %get-tuple-element.15.u_ref, f32[32,8,256]{2,1,0:T(8,128)S(1)} %get-tuple-element.16.v_ref, f32[32,8,256]{2,1,0:T(8,128)S(1)} %get-tuple-element.17.base, ...), custom_call_target="tpu_custom_call" | custom-call | tf_op jit(solution)/shard_map/pallas_call | solution.py:936
